TPU v7x, 8 devices: a whole 2x2x1 slice. The times are simulated.
8 devices in a mesh: data: 1 (over z), pp: 2 (over y), ep: 4 (over x, core).
Axes of the slice: x: 2, y: 2, z: 1, core: 2. Of those that a mesh axis runs over, the one named last changes fastest.
Arguments:
- expert_out: bfloat16 [2, 4, 128, 96, 4096], P('pp', 'data', 'ep')
- expert_ids: int32 [2, 4, 24, 64, 6], P('pp', 'data', 'ep')
- slot_ids: int32 [2, 4, 24, 64, 6], P('pp', 'data', 'ep')
- gate_weights: float32 [2, 4, 24, 64, 6], P('pp', 'data', 'ep')
- residual: bfloat16 [2, 4, 24, 64, 4096], P('pp', 'data', 'ep')
- norm_moe: float32 [2, 4096], P('pp')
- w_gate: bfloat16 [2, 4096, 2816], P('pp')
- w_up: bfloat16 [2, 4096, 2816], P('pp')
- w_down: bfloat16 [2, 2816, 4096], P('pp')
- norm_attn: float32 [2, 4096], P('pp')
- w_query: bfloat16 [2, 4096, 32, 128], P('pp')
- w_key: bfloat16 [2, 4096, 32, 128], P('pp')
- w_value: bfloat16 [2, 4096, 32, 128], P('pp')
- w_out: bfloat16 [2, 32, 128, 4096], P('pp')
Outputs:
- output: bfloat16 [2, 4, 24, 64, 4096], P('pp', 'data', 'ep')
All inputs are finite; a program needn't handle non-finite values.
Results may differ from a plain program's by a relative error of at most 0.0153595.
Values are sent between devices in bfloat16 or wider.
A program may use at most 1.25 GiB of HBM per device.

v0:
```python
import math
import jax
import jax.numpy as jnp
from jax import lax
from jax.sharding import PartitionSpec as P

EPSILON = 1e-6


def rms_norm(tensor, gain):
    values = tensor.astype(jnp.float32)
    inv_rms = lax.rsqrt(jnp.mean(values * values, axis=-1, keepdims=True) + EPSILON)
    return values * inv_rms * gain


def shared_expert(residual, norm_moe, w_gate, w_up, w_down):
    normed = rms_norm(residual, norm_moe).astype(jnp.bfloat16)
    gate_act = jnp.einsum("bld,df->blf", normed, w_gate, preferred_element_type=jnp.float32)
    up_act = jnp.einsum("bld,df->blf", normed, w_up, preferred_element_type=jnp.float32)
    hidden = (jax.nn.silu(gate_act) * up_act).astype(jnp.bfloat16)
    return jnp.einsum("blf,fd->bld", hidden, w_down, preferred_element_type=jnp.float32).astype(jnp.bfloat16)


def gather_combine(row_table, row_ids, kept_mask, gate_weights):
    picked = jnp.take(row_table, row_ids, axis=0, mode="clip")
    weights = jnp.where(kept_mask, gate_weights, 0.0)
    return jnp.sum(picked.astype(jnp.float32) * weights[..., None], axis=-2)


def attention_block(combined, norm_attn, w_query, w_key, w_value, w_out):
    seq_len = combined.shape[1]
    score_scale = 1.0 / math.sqrt(w_query.shape[2])
    normed = rms_norm(combined, norm_attn).astype(jnp.bfloat16)
    queries = jnp.einsum("bld,dhe->blhe", normed, w_query, preferred_element_type=jnp.float32).astype(jnp.bfloat16)
    key_heads = jnp.einsum("bld,dhe->blhe", normed, w_key, preferred_element_type=jnp.float32).astype(jnp.bfloat16)
    value_heads = jnp.einsum("bld,dhe->blhe", normed, w_value, preferred_element_type=jnp.float32).astype(jnp.bfloat16)
    scores = jnp.einsum("bqhe,bkhe->bhqk", queries, key_heads, preferred_element_type=jnp.float32) * score_scale
    causal = jnp.arange(seq_len)[:, None] >= jnp.arange(seq_len)[None, :]
    scores = jnp.where(causal, scores, -1e30)
    attn_probs = jnp.exp(scores - jnp.max(scores, axis=-1, keepdims=True))
    prob_sum = jnp.sum(attn_probs, axis=-1, keepdims=True)
    attn_mixed = jnp.einsum("bhqk,bkhe->bhqe", attn_probs.astype(jnp.bfloat16), value_heads, preferred_element_type=jnp.float32) / prob_sum
    attn_proj = jnp.einsum("cirf,ife->cre", attn_mixed.astype(jnp.bfloat16), w_out, preferred_element_type=jnp.float32).astype(jnp.bfloat16)
    return (combined.astype(jnp.float32) + attn_proj.astype(jnp.float32)).astype(jnp.bfloat16)


def solution(mesh):
    stages = mesh.shape["pp"]
    ep_size = mesh.shape["ep"]
    shift_pairs = [(source, (source + 1) % stages) for source in range(stages)]
    tok_spec = P("pp", "data", "ep", None, None)
    vec_spec = P("pp", None)
    mat_spec = P("pp", None, None)
    head_spec = P("pp", None, None, None)

    def device_step(expert_out, expert_ids, slot_ids, gate_weights, residual, norm_moe, w_gate, w_up, w_down, norm_attn, w_query, w_key, w_value, w_out):
        micro_count = expert_out.shape[1]
        local_experts, slots_total, model_dim = expert_out.shape[2:]
        cap_slots = slots_total // ep_size
        first_slot = lax.axis_index("ep") * cap_slots
        results = []
        for micro_idx in range(micro_count):
            local_out = expert_out[0, micro_idx].reshape(local_experts, ep_size, cap_slots, model_dim)
            received = lax.all_to_all(local_out, "ep", 1, 0, tiled=True)
            row_table = received.reshape(local_experts * ep_size * cap_slots, model_dim)
            slot_here = slot_ids[0, micro_idx]
            kept_mask = slot_here >= 0
            row_ids = expert_ids[0, micro_idx] * cap_slots + jnp.where(kept_mask, slot_here - first_slot, 0)
            routed = gather_combine(row_table, row_ids, kept_mask, gate_weights[0, micro_idx])
            resid_here = residual[0, micro_idx]
            shared = shared_expert(resid_here, norm_moe[0], w_gate[0], w_up[0], w_down[0])
            combined = (resid_here.astype(jnp.float32) + shared.astype(jnp.float32) + routed).astype(jnp.bfloat16)
            incoming = lax.ppermute(combined, "pp", shift_pairs)
            results.append(attention_block(incoming, norm_attn[0], w_query[0], w_key[0], w_value[0], w_out[0]))
        return jnp.stack(results)[None]

    in_specs = (tok_spec,) * 5 + (vec_spec, mat_spec, mat_spec, mat_spec, vec_spec, head_spec, head_spec, head_spec, head_spec)
    return jax.shard_map(device_step, mesh=mesh, in_specs=in_specs, out_specs=tok_spec, check_vma=False)
```

profile of v0, /device:TPU:0, one launch (start us, length us, event | category | flops | bytes accessed | tf_op | source)
XLA Modules:
  0.0 1810.7 jit_solution(14824303923517707072)
XLA Ops:
  0.0 63.1 %fusion.320 = (bf16[1,1,32,96,4096]{4,3,2,1,0:T(8,128)(2,1)}, bf16[1,1,32,96,4096]{4,3,2,1,0:T(8,128)(2,1)}, bf16[1,1,32,96,4096]{4,3,2,1,0:T(8,128)(2,1)}, bf16[1,1,32,96,4096]{4,3,2,1,0:T(8,128)(2,1)}) fusion(bf16[1,4,32,96,4096]{4,3,2,1,0:T(8,128)(2,1)} %param.14), kind=kLoop, calls=%fused_computation.274 | loop fusion | bytes 201326592 | tf_op jit(solution)/shard_map/slice | solution.py:63
  63.1 20.9 %copy.35 = bf16[32,4,24,4096]{3,2,0,1:T(8,128)(2,1)} copy(bf16[32,4,24,4096]{3,2,1,0:T(8,128)(2,1)} %bitcast.296) | data formatting | bytes 50331648 | tf_op jit(solution)/shard_map/reshape;squeeze | solution.py:63
  92.4 20.9 %copy.23 = bf16[32,4,24,4096]{3,2,0,1:T(8,128)(2,1)} copy(bf16[32,4,24,4096]{3,2,1,0:T(8,128)(2,1)} %bitcast.295) | data formatting | bytes 50331648 | tf_op jit(solution)/shard_map/reshape;squeeze | solution.py:63
  113.3 252.7 %all-to-all-done.2 = bf16[32,4,24,4096]{3,2,0,1:T(8,128)(2,1)} async-done(((bf16[32,4,24,4096]{3,2,0,1:T(8,128)(2,1)}), bf16[32,4,24,4096]{3,2,0,1:T(8,128)(2,1)}, u32[]{:S(2)}, u32[]{:S(2)}) %all-to-all-start.2) | async-done | bytes 25165856 | tf_op jit(solution)/shard_map/all_to_all | solution.py:64
  374.4 20.9 %copy.41 = bf16[32,4,24,4096]{3,2,0,1:T(8,128)(2,1)} copy(bf16[32,4,24,4096]{3,2,1,0:T(8,128)(2,1)} %bitcast.294) | data formatting | bytes 50331648 | tf_op jit(solution)/shard_map/reshape;squeeze | solution.py:63
  395.3 251.7 %all-to-all-done = bf16[32,4,24,4096]{3,2,0,1:T(8,128)(2,1)} async-done(((bf16[32,4,24,4096]{3,2,0,1:T(8,128)(2,1)}), bf16[32,4,24,4096]{3,2,0,1:T(8,128)(2,1)}, u32[]{:S(2)}, u32[]{:S(2)}) %all-to-all-start) | async-done | bytes 25165856 | tf_op jit(solution)/shard_map/all_to_all | solution.py:64
  656.0 21.0 %copy.29 = bf16[32,4,24,4096]{3,2,0,1:T(8,128)(2,1)} copy(bf16[32,4,24,4096]{3,2,1,0:T(8,128)(2,1)} %bitcast.293) | data formatting | bytes 50331648 | tf_op jit(solution)/shard_map/reshape;squeeze | solution.py:63
  777.4 151.2 %all-to-all-done.3 = bf16[32,4,24,4096]{3,2,0,1:T(8,128)(2,1)} async-done(((bf16[32,4,24,4096]{3,2,0,1:T(8,128)(2,1)}), bf16[32,4,24,4096]{3,2,0,1:T(8,128)(2,1)}, u32[]{:S(2)}, u32[]{:S(2)}) %all-to-all-start.3) | async-done | bytes 25165856 | tf_op jit(solution)/shard_map/all_to_all | solution.py:64
  977.5 44.0 %gather_fusion.3 = bf16[2304,4096]{1,0:T(8,128)(2,1)} fusion(bf16[3072,4096]{1,0:T(8,128)(2,1)} %bitcast.60, s32[3072]{0:T(1024)S(1)} %pad_clamp_fusion), kind=kCustom, calls=%fused_computation.3 | custom fusion | bytes 37757952 | tf_op jit(solution)/shard_map/jit(_take)/gather | solution.py:25
  1021.4 29.7 %reshape.381 = f32[6,64,6,4096]{3,2,1,0:T(8,128)} reshape(bf16[2304,4096]{1,0:T(8,128)(2,1)} %gather_fusion.3) | data formatting | bytes 56623104 | tf_op jit(solution)/shard_map/convert_element_type | solution.py:27
  1051.2 20.7 %multiply_reduce_fusion = f32[6,64,4096]{2,1,0:T(8,128)S(1)} fusion(f32[6,64,6,4096]{3,2,1,0:T(8,128)} %reshape.381, f32[6,64,6]{2,1,0:T(8,128)S(1)} %copy.46), kind=kLoop, calls=%fused_computation.4 | loop fusion | flops 17301504 | bytes 44049408 | tf_op jit(solution)/shard_map/reduce_sum | solution.py:27
  1090.3 43.6 %gather_fusion = bf16[2304,4096]{1,0:T(8,128)(2,1)} fusion(bf16[3072,4096]{1,0:T(8,128)(2,1)} %bitcast.12, s32[3072]{0:T(1024)S(1)} %copy-done.3), kind=kCustom, calls=%fused_computation | custom fusion | bytes 37757952 | tf_op jit(solution)/shard_map/jit(_take)/gather | solution.py:25
  1133.9 29.8 %reshape.378 = f32[6,64,6,4096]{3,2,1,0:T(8,128)} reshape(bf16[2304,4096]{1,0:T(8,128)(2,1)} %gather_fusion) | data formatting | bytes 56623104 | tf_op jit(solution)/shard_map/convert_element_type | solution.py:27
  1163.6 20.7 %multiply_reduce_fusion.3 = f32[6,64,4096]{2,1,0:T(8,128)S(1)} fusion(f32[6,64,6,4096]{3,2,1,0:T(8,128)} %reshape.378, f32[6,64,6]{2,1,0:T(8,128)S(1)} %copy-done.11), kind=kLoop, calls=%fused_computation.7 | loop fusion | flops 17301504 | bytes 44049408 | tf_op jit(solution)/shard_map/reduce_sum | solution.py:27
  1200.6 43.6 %gather_fusion.2 = bf16[2304,4096]{1,0:T(8,128)(2,1)} fusion(bf16[3072,4096]{1,0:T(8,128)(2,1)} %bitcast.47, s32[3072]{0:T(1024)S(1)} %copy-done.2), kind=kCustom, calls=%fused_computation.2 | custom fusion | bytes 37757952 | tf_op jit(solution)/shard_map/jit(_take)/gather | solution.py:25
  1244.2 29.8 %reshape.380 = f32[6,64,6,4096]{3,2,1,0:T(8,128)} reshape(bf16[2304,4096]{1,0:T(8,128)(2,1)} %gather_fusion.2) | data formatting | bytes 56623104 | tf_op jit(solution)/shard_map/convert_element_type | solution.py:27
  1273.9 21.1 %multiply_reduce_fusion.1 = f32[6,64,4096]{2,1,0:T(8,128)S(1)} fusion(f32[6,64,6,4096]{3,2,1,0:T(8,128)} %reshape.380, f32[6,64,6]{2,1,0:T(8,128)S(1)} %copy-done.10), kind=kLoop, calls=%fused_computation.5 | loop fusion | flops 17301504 | bytes 44049408 | tf_op jit(solution)/shard_map/reduce_sum | solution.py:27
  1313.1 43.6 %gather_fusion.1 = bf16[2304,4096]{1,0:T(8,128)(2,1)} fusion(bf16[3072,4096]{1,0:T(8,128)(2,1)} %bitcast.34, s32[3072]{0:T(1024)S(1)} %copy-done.1), kind=kCustom, calls=%fused_computation.1 | custom fusion | bytes 37757952 | tf_op jit(solution)/shard_map/jit(_take)/gather | solution.py:25
  1356.6 29.9 %reshape.379 = f32[6,64,6,4096]{3,2,1,0:T(8,128)} reshape(bf16[2304,4096]{1,0:T(8,128)(2,1)} %gather_fusion.1) | data formatting | bytes 56623104 | tf_op jit(solution)/shard_map/convert_element_type | solution.py:27
  1386.5 20.7 %multiply_reduce_fusion.2 = f32[6,64,4096]{2,1,0:T(8,128)S(1)} fusion(f32[6,64,6,4096]{3,2,1,0:T(8,128)} %reshape.379, f32[6,64,6]{2,1,0:T(8,128)S(1)} %copy-done.9), kind=kLoop, calls=%fused_computation.6 | loop fusion | flops 17301504 | bytes 44049408 | tf_op jit(solution)/shard_map/reduce_sum | solution.py:27
  1424.7 19.3 %fusion.32 = bf16[6,64,32,128]{3,1,2,0:T(8,128)(2,1)S(1)} fusion(bf16[4096,32,128,1]{2,1,0,3:T(8,128)(2,1)} %bitcast.303, bf16[6,64,4096]{2,1,0:T(8,128)(2,1)} %collective-permute-done.3, f32[6,64]{1,0:T(8,128)S(1)} %add_rsqrt_fusion, f32[4096]{0:T(1024)S(1)} %bitcast.323), kind=kOutput, calls=%fused_computation.40 | convolution fusion | flops 12891193344 | bytes 39863808 | tf_op jit(solution)/shard_map/bld,dhe->blhe/dot_general | solution.py:36
  1450.2 19.1 %fusion.38 = bf16[6,64,32,128]{3,1,2,0:T(8,128)(2,1)S(1)} fusion(bf16[4096,32,128,1]{2,1,0,3:T(8,128)(2,1)} %bitcast.304, bf16[6,64,4096]{2,1,0:T(8,128)(2,1)} %collective-permute-done, f32[4096]{0:T(1024)S(1)} %bitcast.324, f32[6,64]{1,0:T(8,128)S(1)} %add_rsqrt_fusion.6), kind=kOutput, calls=%fused_computation.46 | convolution fusion | flops 12891193344 | bytes 39863808 | tf_op jit(solution)/shard_map/bld,dhe->blhe/dot_general | solution.py:36
  1475.7 19.5 %fusion.34 = bf16[6,64,32,128]{3,1,2,0:T(8,128)(2,1)S(1)} fusion(bf16[4096,32,128,1]{2,1,0,3:T(8,128)(2,1)} %bitcast.305, bf16[6,64,4096]{2,1,0:T(8,128)(2,1)} %collective-permute-done.2, f32[6,64]{1,0:T(8,128)S(1)} %add_rsqrt_fusion.2, f32[4096]{0:T(1024)S(1)} %bitcast.325), kind=kOutput, calls=%fused_computation.42 | convolution fusion | flops 12891193344 | bytes 39863808 | tf_op jit(solution)/shard_map/bld,dhe->blhe/dot_general | solution.py:36
  1499.5 18.9 %fusion.36 = bf16[6,64,32,128]{3,1,2,0:T(8,128)(2,1)S(1)} fusion(bf16[4096,32,128,1]{2,1,0,3:T(8,128)(2,1)} %bitcast.306, bf16[6,64,4096]{2,1,0:T(8,128)(2,1)S(1)} %collective-permute-done.1, f32[6,64]{1,0:T(8,128)S(1)} %add_rsqrt_fusion.4, f32[4096]{0:T(1024)S(1)} %bitcast.326), kind=kOutput, calls=%fused_computation.44 | convolution fusion | flops 12891193344 | bytes 39863808 | tf_op jit(solution)/shard_map/bld,dhe->blhe/dot_general | solution.py:36
  1522.2 19.1 %fusion.40 = bf16[6,64,32,128]{3,1,2,0:T(8,128)(2,1)S(1)} fusion(bf16[4096,32,128,1]{2,1,0,3:T(8,128)(2,1)} %bitcast.307, bf16[6,64,4096]{2,1,0:T(8,128)(2,1)} %collective-permute-done.3, f32[6,64]{1,0:T(8,128)S(1)} %add_rsqrt_fusion, f32[4096]{0:T(1024)S(1)} %bitcast.327), kind=kOutput, calls=%fused_computation.48 | convolution fusion | flops 12891193344 | bytes 39863808 | tf_op jit(solution)/shard_map/bld,dhe->blhe/dot_general | solution.py:35
  1541.2 19.1 %fusion.48 = bf16[6,64,32,128]{3,1,2,0:T(8,128)(2,1)S(1)} fusion(bf16[4096,32,128,1]{2,1,0,3:T(8,128)(2,1)} %bitcast.311, bf16[6,64,4096]{2,1,0:T(8,128)(2,1)} %collective-permute-done.3, f32[6,64]{1,0:T(8,128)S(1)} %add_rsqrt_fusion, f32[4096]{0:T(1024)S(1)} %bitcast.328), kind=kOutput, calls=%fused_computation.56 | convolution fusion | flops 12891193344 | bytes 39863808 | tf_op jit(solution)/shard_map/bld,dhe->blhe/dot_general | solution.py:34
  1564.8 19.3 %fusion.42 = bf16[6,64,32,128]{3,1,2,0:T(8,128)(2,1)S(1)} fusion(bf16[4096,32,128,1]{2,1,0,3:T(8,128)(2,1)} %bitcast.308, bf16[6,64,4096]{2,1,0:T(8,128)(2,1)} %collective-permute-done.2, f32[6,64]{1,0:T(8,128)S(1)} %add_rsqrt_fusion.2, f32[4096]{0:T(1024)S(1)} %bitcast.329), kind=kOutput, calls=%fused_computation.50 | convolution fusion | flops 12891193344 | bytes 39863808 | tf_op jit(solution)/shard_map/bld,dhe->blhe/dot_general | solution.py:35
  1584.1 19.1 %fusion.50 = bf16[6,64,32,128]{3,1,2,0:T(8,128)(2,1)S(1)} fusion(bf16[4096,32,128,1]{2,1,0,3:T(8,128)(2,1)} %bitcast.312, bf16[6,64,4096]{2,1,0:T(8,128)(2,1)} %collective-permute-done.2, f32[6,64]{1,0:T(8,128)S(1)} %add_rsqrt_fusion.2, f32[4096]{0:T(1024)S(1)} %bitcast.330), kind=kOutput, calls=%fused_computation.58 | convolution fusion | flops 12891193344 | bytes 39863808 | tf_op jit(solution)/shard_map/bld,dhe->blhe/dot_general | solution.py:34
  1607.6 19.5 %fusion.46 = bf16[6,64,32,128]{3,1,2,0:T(8,128)(2,1)S(1)} fusion(bf16[4096,32,128,1]{2,1,0,3:T(8,128)(2,1)} %bitcast.309, bf16[6,64,4096]{2,1,0:T(8,128)(2,1)} %collective-permute-done, f32[4096]{0:T(1024)S(1)} %bitcast.331, f32[6,64]{1,0:T(8,128)S(1)} %copy-done.17), kind=kOutput, calls=%fused_computation.54 | convolution fusion | flops 12891193344 | bytes 39863808 | tf_op jit(solution)/shard_map/bld,dhe->blhe/dot_general | solution.py:35
  1627.1 19.1 %fusion.54 = bf16[6,64,32,128]{3,1,2,0:T(8,128)(2,1)S(1)} fusion(bf16[4096,32,128,1]{2,1,0,3:T(8,128)(2,1)} %bitcast.313, bf16[6,64,4096]{2,1,0:T(8,128)(2,1)} %collective-permute-done, f32[4096]{0:T(1024)S(1)} %bitcast.332, f32[6,64]{1,0:T(8,128)S(1)} %copy-done.17), kind=kOutput, calls=%fused_computation.62 | convolution fusion | flops 12891193344 | bytes 39863808 | tf_op jit(solution)/shard_map/bld,dhe->blhe/dot_general | solution.py:34
  1650.7 19.7 %fusion.44 = bf16[6,64,32,128]{3,1,2,0:T(8,128)(2,1)} fusion(bf16[4096,32,128,1]{2,1,0,3:T(8,128)(2,1)} %bitcast.310, bf16[6,64,4096]{2,1,0:T(8,128)(2,1)S(1)} %copy-done.5, f32[6,64]{1,0:T(8,128)S(1)} %copy-done.19, f32[4096]{0:T(1024)S(1)} %bitcast.333), kind=kOutput, calls=%fused_computation.52 | convolution fusion | flops 12891193344 | bytes 39863808 | tf_op jit(solution)/shard_map/bld,dhe->blhe/dot_general | solution.py:35
  1670.4 19.5 %fusion.52 = bf16[6,64,32,128]{3,1,2,0:T(8,128)(2,1)} fusion(bf16[4096,32,128,1]{2,1,0,3:T(8,128)(2,1)} %bitcast.314, bf16[6,64,4096]{2,1,0:T(8,128)(2,1)S(1)} %copy-done.5, f32[6,64]{1,0:T(8,128)S(1)} %copy-done.19, f32[4096]{0:T(1024)S(1)} %bitcast.334), kind=kOutput, calls=%fused_computation.60 | convolution fusion | flops 12891193344 | bytes 39863808 | tf_op jit(solution)/shard_map/bld,dhe->blhe/dot_general | solution.py:34
  (145 shorter events, 399.5 us)
Async XLA Ops:
  84.0 282.0 %all-to-all-start.2 = ((bf16[32,4,24,4096]{3,2,0,1:T(8,128)(2,1)}), bf16[32,4,24,4096]{3,2,0,1:T(8,128)(2,1)}, u32[]{:S(2)}, u32[]{:S(2)}) async-start(bf16[32,4,24,4096]{3,2,0,1:T(8,128)(2,1)} %copy.35), calls=%async_computation.2 | async-start | bytes 50331648 | tf_op jit(solution)/shard_map/all_to_all | solution.py:64
  366.0 281.0 %all-to-all-start = ((bf16[32,4,24,4096]{3,2,0,1:T(8,128)(2,1)}), bf16[32,4,24,4096]{3,2,0,1:T(8,128)(2,1)}, u32[]{:S(2)}, u32[]{:S(2)}) async-start(bf16[32,4,24,4096]{3,2,0,1:T(8,128)(2,1)} %copy.23), calls=%async_computation | async-start | bytes 50331648 | tf_op jit(solution)/shard_map/all_to_all | solution.py:64
  647.0 281.5 %all-to-all-start.3 = ((bf16[32,4,24,4096]{3,2,0,1:T(8,128)(2,1)}), bf16[32,4,24,4096]{3,2,0,1:T(8,128)(2,1)}, u32[]{:S(2)}, u32[]{:S(2)}) async-start(bf16[32,4,24,4096]{3,2,0,1:T(8,128)(2,1)} %copy.41), calls=%async_computation.3 | async-start | bytes 50331648 | tf_op jit(solution)/shard_map/all_to_all | solution.py:64
  677.0 6.1 copy-start.12
  677.0 6.2 copy-start.13
  677.0 6.3 copy-start.14
  677.0 6.4 copy-start.20
  677.0 23.3 %slice-start.4 = ((s8[12582912]{0:T(1024)(128)(4,1)}), s8[4194304]{0:T(1024)(128)(4,1)S(1)}, s32[]{:S(2)}) async-start(s8[12582912]{0:T(1024)(128)(4,1)} %bitcast.301), calls=%async_computation.8 | async-start | bytes 8388608
  683.4 16.9 slice-start.5
  683.4 16.9 slice-start.6
  928.6 384.5 %all-to-all-start.1 = ((bf16[32,4,24,4096]{3,2,0,1:T(8,128)(2,1)}), bf16[32,4,24,4096]{3,2,0,1:T(8,128)(2,1)}, u32[]{:S(2)}, u32[]{:S(2)}) async-start(bf16[32,4,24,4096]{3,2,0,1:T(8,128)(2,1)} %copy.29), calls=%async_computation.1 | async-start | bytes 50331648 | tf_op jit(solution)/shard_map/all_to_all | solution.py:64
  1071.8 18.5 %copy-start.3 = (s32[3072]{0:T(1024)S(1)}, s32[3072]{0:T(1024)}, u32[]{:S(2)}) copy-start(s32[3072]{0:T(1024)} %pad_clamp_fusion.3) | copy-start | bytes 36868
  1087.9 334.2 %collective-permute-start.3 = (bf16[6,64,4096]{2,1,0:T(8,128)(2,1)}, bf16[6,64,4096]{2,1,0:T(8,128)(2,1)}, u32[]{:S(2)}, u32[]{:S(2)}) collective-permute-start(bf16[6,64,4096]{2,1,0:T(8,128)(2,1)} %fusion.81), channel_id=1, source_target_pairs={{0,4},{4,0},{1,5},{5,1},{2,6},{6,2},{3,7},{7,3}} | collective-permute-start | bytes 9437192 | tf_op jit(solution)/shard_map/ppermute | solution.py:73
  1133.9 29.8 %copy-start.11 = (f32[6,64,6]{2,1,0:T(8,128)S(1)}, f32[6,64,6]{2,1,0:T(8,128)}, u32[]{:S(2)}) copy-start(f32[6,64,6]{2,1,0:T(8,128)} %copy.28) | copy-start | bytes 27652
  1184.3 16.3 copy-start.2
  1200.5 247.1 %collective-permute-start = (bf16[6,64,4096]{2,1,0:T(8,128)(2,1)}, bf16[6,64,4096]{2,1,0:T(8,128)(2,1)}, u32[]{:S(2)}, u32[]{:S(2)}) collective-permute-start(bf16[6,64,4096]{2,1,0:T(8,128)(2,1)} %fusion.66), channel_id=1, source_target_pairs={{0,4},{4,0},{1,5},{5,1},{2,6},{6,2},{3,7},{7,3}} | collective-permute-start | bytes 9437192 | tf_op jit(solution)/shard_map/ppermute | solution.py:73
  1244.2 29.8 %copy-start.10 = (f32[6,64,6]{2,1,0:T(8,128)S(1)}, f32[6,64,6]{2,1,0:T(8,128)}, u32[]{:S(2)}) copy-start(f32[6,64,6]{2,1,0:T(8,128)} %copy.40) | copy-start | bytes 27652
  1295.0 18.1 copy-start.1
  1311.1 162.0 %collective-permute-start.2 = (bf16[6,64,4096]{2,1,0:T(8,128)(2,1)}, bf16[6,64,4096]{2,1,0:T(8,128)(2,1)}, u32[]{:S(2)}, u32[]{:S(2)}) collective-permute-start(bf16[6,64,4096]{2,1,0:T(8,128)(2,1)} %fusion.76), channel_id=1, source_target_pairs={{0,4},{4,0},{1,5},{5,1},{2,6},{6,2},{3,7},{7,3}} | collective-permute-start | bytes 9437192 | tf_op jit(solution)/shard_map/ppermute | solution.py:73
  1356.6 29.9 %copy-start.9 = (f32[6,64,6]{2,1,0:T(8,128)S(1)}, f32[6,64,6]{2,1,0:T(8,128)}, u32[]{:S(2)}) copy-start(f32[6,64,6]{2,1,0:T(8,128)} %copy.34) | copy-start | bytes 27652
  1407.2 17.5 copy-start.21
  1422.0 76.8 %collective-permute-start.1 = (bf16[6,64,4096]{2,1,0:T(8,128)(2,1)S(1)}, bf16[6,64,4096]{2,1,0:T(8,128)(2,1)S(1)}, u32[]{:S(2)}, u32[]{:S(2)}) collective-permute-start(bf16[6,64,4096]{2,1,0:T(8,128)(2,1)S(1)} %fusion.71), channel_id=1, source_target_pairs={{0,4},{4,0},{1,5},{5,1},{2,6},{6,2},{3,7},{7,3}} | collective-permute-start | bytes 9437192 | tf_op jit(solution)/shard_map/ppermute | solution.py:73
  1450.2 19.1 %copy-start.16 = (f32[6,64]{1,0:T(8,128)}, f32[6,64]{1,0:T(8,128)S(1)}, u32[]{:S(2)}) copy-start(f32[6,64]{1,0:T(8,128)S(1)} %add_rsqrt_fusion.6) | copy-start | bytes 4612
  1498.8 19.6 %copy-start.4 = (bf16[6,64,4096]{2,1,0:T(8,128)(2,1)}, bf16[6,64,4096]{2,1,0:T(8,128)(2,1)S(1)}, u32[]{:S(2)}) copy-start(bf16[6,64,4096]{2,1,0:T(8,128)(2,1)S(1)} %collective-permute-done.1) | copy-start | bytes 9437188
  1499.5 18.9 %copy-start.18 = (f32[6,64]{1,0:T(8,128)}, f32[6,64]{1,0:T(8,128)S(1)}, u32[]{:S(2)}) copy-start(f32[6,64]{1,0:T(8,128)S(1)} %add_rsqrt_fusion.4) | copy-start | bytes 4612
  1627.1 19.1 %copy-start.15 = (pred[64,64]{0,1:T(8,128)(4,1)S(1)}, pred[64,64]{0,1:T(8,128)(4,1)}, u32[]{:S(2)}) copy-start(pred[64,64]{0,1:T(8,128)(4,1)} %iota_compare_fusion) | copy-start | bytes 12292
  1650.7 39.2 %slice-start = ((s8[6291456]{0:T(1024)(128)(4,1)}), s8[4194304]{0:T(1024)(128)(4,1)S(1)}, s32[]{:S(2)}) async-start(s8[6291456]{0:T(1024)(128)(4,1)} %bitcast.297), calls=%async_computation.4 | async-start | bytes 8388608
  1670.3 19.5 %slice-start.1 = ((s8[6291456]{0:T(1024)(128)(4,1)}), s8[2097152]{0:T(1024)(128)(4,1)S(1)}, s32[]{:S(2)}) async-start(s8[6291456]{0:T(1024)(128)(4,1)} %bitcast.297), calls=%async_computation.5 | async-start | bytes 4194304
  1704.0 8.0 copy-start
  1712.0 8.2 copy-start.6
  1712.0 13.4 slice-start.2
  1733.6 17.9 copy-start.23
  (7 other events, 31.9 us)
where the time goes:
time: 1820 us; the launch traced here: 1810 us
  waiting for transfers between devices  656 us (36%)
  matrix products  542 us (30%)
  local copies, waits for them, and re-layouts  459 us (25%)
  other arithmetic  114 us (6%)
  starting transfers between devices  38.7 us (2%)
    all_to_all x4, waiting for transfers between devices, device_step(): received = lax.all_to_all(local_out, 'ep', 1, 0, tiled=True)  656 us
    gather x4, local copies, waits for them, and re-layouts, gather_combine(): picked = jnp.take(row_table, row_ids, axis=0, mode='clip')  175 us
    convert_element_type x4, local copies, waits for them, and re-layouts, gather_combine(): return jnp.sum(picked.astype(jnp.float32) * weights[..., None], axis=-2)  119 us
    another operation x4, local copies, waits for them, and re-layouts, device_step(): expert_out[0, micro_idx]  83.7 us
    reduce_sum x4, other arithmetic, gather_combine(): return jnp.sum(picked.astype(jnp.float32) * weights[..., None], axis=-2)  83 us
    dot_general x4, matrix products, attention_block(): jnp.einsum('bld,dhe->blhe', normed, w_key, preferred_element_type=jnp.flo...  77.5 us
    dot_general x4, matrix products, attention_block(): jnp.einsum('bld,dhe->blhe', normed, w_query, preferred_element_type=jnp.f...  76.8 us
    dot_general x4, matrix products, attention_block(): jnp.einsum('bld,dhe->blhe', normed, w_value, preferred_element_type=jnp.f...  76.7 us
  transfers between devices with their start and end apart: 8, of which 3 were waited for; matrix products, arithmetic and copies ran while one was open for 40% of the time, Pallas kernels for 0%

commit v1 on v0

v1 whole, which is shorter than its diff:
```python
import math
import jax
import jax.numpy as jnp
from jax import lax
from jax.experimental import pallas as pl
from jax.experimental.pallas import tpu as pltpu
from jax.sharding import PartitionSpec as P

EPSILON = 1e-6
LANES = 128
CHUNKS = (2, 2, 2, 3)
ROWS = 64
VMEM_LIMIT = 60 << 20
ANY = pl.BlockSpec(memory_space=pl.ANY)


def normalize(blocks, gain, deps=()):
    dim = blocks[0].shape[1]
    step = blocks[0].shape[0]
    counts = [block.shape[0] // step for block in blocks]
    starts = [sum(counts[:c]) for c in range(len(blocks))]
    total = sum(counts)

    def body(*refs):
        sources, gain_ref, out_ref = refs[:len(blocks)], refs[len(blocks)], refs[-1]
        s = pl.program_id(0)
        for ref, start, count in zip(sources, starts, counts):
            @pl.when((s >= start) & (s < start + count))
            def _():
                values = ref[...].astype(jnp.float32)
                inv_rms = lax.rsqrt(jnp.mean(values * values, axis=-1, keepdims=True) + EPSILON)
                out_ref[...] = (values * inv_rms * gain_ref[...]).astype(jnp.bfloat16)

    def spec(start, count):
        return pl.BlockSpec((step, dim), lambda s: (jnp.clip(s - start, 0, count - 1), 0))

    return pl.pallas_call(
        body,
        out_shape=jax.ShapeDtypeStruct((total * step, dim), jnp.bfloat16),
        grid=(total,),
        in_specs=[spec(*pair) for pair in zip(starts, counts)] + [pl.BlockSpec((1, dim), lambda s: (0, 0))] + [ANY] * len(deps),
        out_specs=pl.BlockSpec((step, dim), lambda s: (s, 0)),
        cost_estimate=pl.CostEstimate(flops=1_000_000_000, bytes_accessed=4 * total * step * dim, transcendentals=0),
        name="normalize",
    )(*blocks, gain, *deps)


def gated_hidden(residual, part, parts, gain, w_gate, w_up, deps=()):
    rows, dim = residual.shape[0] // parts, residual.shape[1]
    width = w_gate.shape[1]
    block = 384
    cols = 256

    def gated(res_ref, gain_ref, gate_ref, up_ref, *rest):
        hidden_ref, normed = rest[-2:]

        @pl.when(pl.program_id(0) == 0)
        def _():
            def scale_rows(r, carry):
                at = pl.ds(pl.multiple_of(r * ROWS, ROWS), ROWS)
                values = res_ref[at, :].astype(jnp.float32)
                inv_rms = lax.rsqrt(jnp.mean(values * values, axis=-1, keepdims=True) + EPSILON)
                normed[at, :] = (values * inv_rms * gain_ref[...]).astype(jnp.bfloat16)
                return carry

            lax.fori_loop(0, rows // ROWS, scale_rows, 0)

        def product(r, carry):
            at = pl.ds(pl.multiple_of(r * block, block), block)
            gate_act = jnp.dot(normed[at, :], gate_ref[...], preferred_element_type=jnp.float32)
            up_act = jnp.dot(normed[at, :], up_ref[...], preferred_element_type=jnp.float32)
            hidden_ref[at, :] = (jax.nn.silu(gate_act) * up_act).astype(jnp.bfloat16)
            return carry

        lax.fori_loop(0, rows // block, product, 0)

    return pl.pallas_call(
        gated,
        out_shape=jax.ShapeDtypeStruct((rows, width), jnp.bfloat16),
        grid=(width // cols,),
        in_specs=[
            pl.BlockSpec((rows, dim), lambda n: (part, 0), pipeline_mode=pl.Buffered(1)),
            pl.BlockSpec((1, dim), lambda n: (0, 0)),
            pl.BlockSpec((dim, cols), lambda n: (0, n)),
            pl.BlockSpec((dim, cols), lambda n: (0, n)),
        ] + [ANY] * len(deps),
        out_specs=pl.BlockSpec((rows, cols), lambda n: (0, n)),
        scratch_shapes=[pltpu.VMEM((rows, dim), jnp.bfloat16)],
        compiler_params=pltpu.CompilerParams(vmem_limit_bytes=VMEM_LIMIT),
        cost_estimate=pl.CostEstimate(flops=4 * rows * dim * width, bytes_accessed=4 * dim * width, transcendentals=0),
        name="gated",
    )(residual, gain, w_gate, w_up, *deps)


def down_product(hidden, w_down, deps=()):
    rows, width = hidden.shape
    dim = w_down.shape[1]
    block = 384
    out_cols = 512

    def down(hidden_ref, w_ref, *rest):
        out_ref = rest[-1]

        def product(r, carry):
            at = pl.ds(pl.multiple_of(r * block, block), block)
            out_ref[at, :] = jnp.dot(hidden_ref[at, :], w_ref[...], preferred_element_type=jnp.float32).astype(jnp.bfloat16)
            return carry

        lax.fori_loop(0, rows // block, product, 0)

    return pl.pallas_call(
        down,
        out_shape=jax.ShapeDtypeStruct((rows, dim), jnp.bfloat16),
        grid=(dim // out_cols,),
        in_specs=[
            pl.BlockSpec((rows, width), lambda n: (0, 0), pipeline_mode=pl.Buffered(1)),
            pl.BlockSpec((width, out_cols), lambda n: (0, n)),
        ] + [ANY] * len(deps),
        out_specs=pl.BlockSpec((rows, out_cols), lambda n: (0, n)),
        compiler_params=pltpu.CompilerParams(vmem_limit_bytes=VMEM_LIMIT),
        cost_estimate=pl.CostEstimate(flops=2 * rows * dim * width, bytes_accessed=2 * dim * width, transcendentals=0),
        name="down",
    )(hidden, w_down, *deps)


def attend(queries, keys, values, row_block, blocks, w_out, micro, micro_count, seq_len, head_dim, previous=None, deps=()):
    width = queries.shape[1]
    dim = w_out.shape[1]
    cols = 1024
    group = 4
    pair = 2 * seq_len
    core_steps = width // (group * head_dim)
    scale = 1.0 / math.sqrt(head_dim)
    sizes = [block.shape[0] for block in blocks]
    starts = [sum(sizes[:c]) for c in range(len(sizes))]
    tokens = sum(sizes)

    def body(q_ref, k_ref, v_ref, w_ref, *rest):
        y_refs = rest[:len(blocks)]
        out_ref, mixed = rest[-2], rest[-1]
        s = pl.program_id(0)

        @pl.when(s < core_steps)
        def _():
            row = lax.broadcasted_iota(jnp.int32, (pair, pair), 0)
            col = lax.broadcasted_iota(jnp.int32, (pair, pair), 1)
            visible = (row >= col) & ((row < seq_len) | (col >= seq_len))
            tiles = [(slice(p * pair, (p + 1) * pair), slice(h * head_dim, (h + 1) * head_dim), h) for h in range(group) for p in range(tokens // pair)]
            scores = [lax.dot_general(q_ref[r, c], k_ref[r, c], (((1,), (1,)), ((), ())), preferred_element_type=jnp.float32) * scale for r, c, _ in tiles]
            scores = [jnp.where(visible, score, -1e30) for score in scores]
            probs = [jnp.exp(score - jnp.max(score, axis=-1, keepdims=True)) for score in scores]
            totals = [jnp.sum(prob, axis=-1, keepdims=True) for prob in probs]
            outs = [jnp.dot(prob.astype(jnp.bfloat16), v_ref[r, c], preferred_element_type=jnp.float32) for prob, (r, c, _) in zip(probs, tiles)]
            for out, total, (r, _, h) in zip(outs, totals, tiles):
                mixed[r, pl.ds(pl.multiple_of((s * group + h) * head_dim, head_dim), head_dim)] = (out / total).astype(jnp.bfloat16)

        @pl.when(s >= core_steps)
        def _():
            proj = jnp.dot(mixed[...], w_ref[...], preferred_element_type=jnp.float32).astype(jnp.bfloat16)
            for ref, start, size in zip(y_refs, starts, sizes):
                part = proj[start:start + size].astype(jnp.float32)
                out_ref[0, start:start + size, :] = (ref[...].astype(jnp.float32) + part).astype(jnp.bfloat16)

    core_spec = pl.BlockSpec((tokens, group * head_dim), lambda s: (row_block, jnp.minimum(s, core_steps - 1)))
    tail = lambda s: jnp.maximum(s - core_steps, 0)
    extra = list(deps) + ([] if previous is None else [previous])
    aliases = {} if previous is None else {4 + len(blocks) + len(deps): 0}
    return pl.pallas_call(
        body,
        out_shape=jax.ShapeDtypeStruct((micro_count, tokens, dim), jnp.bfloat16),
        grid=(core_steps + dim // cols,),
        in_specs=[core_spec, core_spec, core_spec, pl.BlockSpec((width, cols), lambda s: (0, tail(s)))]
        + [pl.BlockSpec((size, cols), lambda s: (0, tail(s))) for size in sizes] + [ANY] * len(extra),
        out_specs=pl.BlockSpec((1, tokens, cols), lambda s: (micro, 0, tail(s))),
        scratch_shapes=[pltpu.VMEM((tokens, width), jnp.bfloat16)],
        input_output_aliases=aliases,
        compiler_params=pltpu.CompilerParams(vmem_limit_bytes=VMEM_LIMIT),
        cost_estimate=pl.CostEstimate(flops=2 * tokens * width * dim, bytes_accessed=2 * width * dim, transcendentals=0),
        name="attend",
    )(queries, keys, values, w_out, *blocks, *extra)


def pick_rows(expert_out, picks, cap, deps=()):
    experts, _, dim = expert_out.shape[2:]
    step = 8
    count = len(picks)

    def body(owners_ref, *refs):
        for source_ref, out_ref in zip(refs[:count], refs[-count:]):
            out_ref[...] = source_ref[0, 0]

    def source(which, micro):
        return pl.BlockSpec((1, 1, step, cap, dim), lambda s, o: (0, micro, s, o[which], 0))

    return pl.pallas_call(
        body,
        out_shape=[jax.ShapeDtypeStruct((experts, cap, dim), expert_out.dtype)] * count,
        grid_spec=pltpu.PrefetchScalarGridSpec(
            num_scalar_prefetch=1,
            grid=(experts // step,),
            in_specs=[source(which, micro) for which, (micro, _) in enumerate(picks)] + [ANY] * len(deps),
            out_specs=[pl.BlockSpec((step, cap, dim), lambda s, o: (s, 0, 0))] * count,
        ),
        cost_estimate=pl.CostEstimate(flops=2_000_000_000 * count, bytes_accessed=4 * experts * cap * dim * count, transcendentals=0),
        name="pick",
    )(jnp.stack([owner for _, owner in picks]).astype(jnp.int32), *([expert_out] * count), *deps)


def chip_partial(expert_out, sibling_rows, micro, owner, rows, gates, tokens, top_k, chunks, deps=()):
    experts, cap, dim = sibling_rows.shape
    step = 16
    tiles = dim // LANES
    half = experts // step
    pitch = 2 * experts * cap + 1
    parts = tokens // chunks // ROWS

    def body(owner_ref, rows_ref, gates_ref, own_ref, sib_ref, *rest):
        outs, table = rest[len(deps):-1], rest[-1]
        s = pl.program_id(0)

        def put(ref, base):
            for e in range(step):
                for j in range(tiles):
                    table[pl.ds(j * pitch + base + e * cap, cap), :] = ref[e, :, j * LANES:(j + 1) * LANES].astype(jnp.float32)

        base = pl.multiple_of(s * (step * cap), 8)

        @pl.when(s < half)
        def _():
            put(own_ref.at[0, 0], base)

        @pl.when((s >= half) & (s < 2 * half))
        def _():
            put(sib_ref, base)

        for c, out_ref in enumerate(outs):
            first = 2 * half + c * parts

            @pl.when((s >= first) & (s < first + parts))
            def _():
                def token(t, carry):
                    acc = None
                    for j in range(top_k):
                        at = ((s - 2 * half) * ROWS + t) * top_k + j
                        term = table[pl.ds(rows_ref[at], tiles, stride=pitch), :] * gates_ref[at]
                        acc = term if acc is None else acc + term
                    out_ref[pl.ds(pl.multiple_of(t * tiles, tiles), tiles), :] = acc
                    return carry

                lax.fori_loop(0, ROWS, token, 0, unroll=4)

    def out_spec(c):
        return pl.BlockSpec((ROWS * tiles, LANES), lambda s, o, r, g: (jnp.clip(s - 2 * half - c * parts, 0, parts - 1), 0))

    return pl.pallas_call(
        body,
        out_shape=[jax.ShapeDtypeStruct((parts * ROWS * tiles, LANES), jnp.float32)] * chunks,
        grid_spec=pltpu.PrefetchScalarGridSpec(
            num_scalar_prefetch=3,
            grid=(2 * half + chunks * parts,),
            in_specs=[
                pl.BlockSpec((1, 1, step, cap, dim), lambda s, o, r, g: (0, micro, jnp.minimum(s, half - 1), o[0], 0)),
                pl.BlockSpec((step, cap, dim), lambda s, o, r, g: (jnp.clip(s - half, 0, half - 1), 0, 0)),
            ] + [ANY] * len(deps),
            out_specs=[out_spec(c) for c in range(chunks)],
            scratch_shapes=[pltpu.VMEM((tiles * pitch, LANES), jnp.float32)],
        ),
        compiler_params=pltpu.CompilerParams(vmem_limit_bytes=VMEM_LIMIT),
        cost_estimate=pl.CostEstimate(flops=8_000_000_000, bytes_accessed=3 * experts * cap * dim * 2, transcendentals=0),
        name="combine",
    )(owner, rows, gates, expert_out, sibling_rows, *deps)


def combine_chunk(own_part, far_part, residual, shared, start, sh_start, deps=()):
    dim = residual.shape[1]
    tiles = dim // LANES
    chunk = own_part.shape[0] // tiles
    pitch = ROWS + 2

    def body(own_ref, far_ref, res_ref, sh_ref, *rest):
        out_ref, planes = rest[-2:]

        def token(t, carry):
            at = pl.ds(pl.multiple_of(t * tiles, tiles), tiles)
            planes[pl.ds(t, tiles, stride=pitch), :] = own_ref[at, :] + far_ref[at, :]
            return carry

        lax.fori_loop(0, ROWS, token, 0, unroll=8)
        for j in range(tiles):
            at = slice(j * LANES, (j + 1) * LANES)
            total = res_ref[:, at].astype(jnp.float32) + sh_ref[:, at].astype(jnp.float32) + planes[j * pitch:j * pitch + ROWS, :]
            out_ref[:, at] = total.astype(jnp.bfloat16)

    part_spec = pl.BlockSpec((ROWS * tiles, LANES), lambda s: (s, 0))
    rows_from = lambda first: pl.BlockSpec((ROWS, dim), lambda s: (first // ROWS + s, 0))
    return pl.pallas_call(
        body,
        out_shape=jax.ShapeDtypeStruct((chunk, dim), jnp.bfloat16),
        grid=(chunk // ROWS,),
        in_specs=[part_spec, part_spec, rows_from(start), rows_from(sh_start)] + [ANY] * len(deps),
        out_specs=pl.BlockSpec((ROWS, dim), lambda s: (s, 0)),
        scratch_shapes=[pltpu.VMEM((tiles * pitch, LANES), jnp.float32)],
        cost_estimate=pl.CostEstimate(flops=1_000_000_000, bytes_accessed=14 * chunk * dim, transcendentals=0),
        name="finish",
    )(own_part, far_part, residual, shared, *deps)


def solution(mesh):
    stages = mesh.shape["pp"]
    ep_size = mesh.shape["ep"]
    shift_pairs = [(source, (source + 1) % stages) for source in range(stages)]
    core_pairs = [(source, source ^ 1) for source in range(ep_size)]
    chip_pairs = [(source, (source + 2) % ep_size) for source in range(ep_size)]
    tok_spec = P("pp", "data", "ep", None, None)
    vec_spec = P("pp", None)
    mat_spec = P("pp", None, None)
    head_spec = P("pp", None, None, None)

    def device_step(expert_out, expert_ids, slot_ids, gate_weights, residual, norm_moe, w_gate, w_up, w_down, norm_attn, w_query, w_key, w_value, w_out):
        micro_count, local_experts, slots_total, dim = expert_out.shape[1:]
        seqs, seq_len, top_k = expert_ids.shape[2:]
        tokens = seqs * seq_len
        cap = slots_total // ep_size
        me = lax.axis_index("ep")
        chip, core = me // 2, me % 2
        far = (me + 2) % ep_size
        as_owner = lambda who: jnp.reshape(who, (1,)).astype(jnp.int32)

        home = expert_ids[0] // local_experts
        slot = slot_ids[0]
        row_here = (expert_ids[0] % local_experts) * cap + (slot - me * cap)

        def routing(on_chip):
            usable = (slot >= 0) & (home // 2 == on_chip)
            row = row_here + jnp.where(home % 2 == core, 0, local_experts * cap)
            flat = (micro_count, tokens * top_k)
            return jnp.where(usable, row, 0).reshape(flat), jnp.where(usable, gate_weights[0], 0.0).reshape(flat)

        own_rows, own_gates = routing(chip)
        send_rows, send_gates = routing(1 - chip)
        far_meta = lax.ppermute(jnp.stack([send_rows.astype(jnp.float32), send_gates]), "ep", chip_pairs)
        far_rows, far_gates = far_meta[0].astype(jnp.int32), far_meta[1]

        to_far = lambda m: (m, far ^ 1)
        to_own = lambda m: (m, me ^ 1)
        pick_plan = ([to_far(0)], [to_far(1)], [to_far(2), to_own(0)], [to_far(3), to_own(1)], [to_own(2), to_own(3)])
        from_sibling = []

        def exchange(step, deps):
            picked = pick_rows(expert_out, pick_plan[step], cap, deps)
            from_sibling.append([lax.ppermute(rows, "ep", core_pairs) for rows in picked])
            return (picked[-1],)

        last = exchange(1, exchange(0, ()))
        arrived = []
        for m in range(micro_count):
            parts = chip_partial(expert_out, from_sibling[m][0], m, as_owner(far), far_rows[m], far_gates[m], tokens, top_k, CHUNKS[m], last)
            last = (parts[0],)
            arrived.append([])
            for part in parts:
                arrived[m].append(lax.ppermute(part, "ep", chip_pairs))
            if m + 2 < len(pick_plan):
                last = exchange(m + 2, last)
        own_sib = [from_sibling[2][1], from_sibling[3][1], *from_sibling[4]]

        flat_resid = residual.reshape(micro_count * tokens, dim)
        heads_width = w_query.shape[2] * w_query.shape[3]
        flat = lambda weight: weight[0].reshape(dim, heads_width)

        def own(m, deps):
            return chip_partial(expert_out, own_sib[m], m, as_owner(me), own_rows[m], own_gates[m], tokens, top_k, CHUNKS[m], deps)

        halves = 2
        half_tokens = micro_count * tokens // halves
        hidden_half = lambda part, deps: gated_hidden(flat_resid, part, halves, norm_moe, w_gate[0], w_up[0], deps)
        shared = [down_product(hidden_half(0, last), w_down[0])]
        here = [None] * micro_count
        pieces = [[] for _ in range(micro_count)]

        def finish(m, c, deps):
            chunk = tokens // CHUNKS[m]
            start = m * tokens + c * chunk
            combined = combine_chunk(here[m][c], arrived[m][c], flat_resid, shared[start // half_tokens], start, start % half_tokens, deps)
            pieces[m].append(lax.ppermute(combined, "pp", shift_pairs))
            return (combined,)

        def project(micros, deps):
            normed = normalize([piece for m in micros for piece in pieces[m]], norm_attn, deps)
            return [jnp.dot(normed, flat(weight), preferred_element_type=jnp.float32).astype(jnp.bfloat16) for weight in (w_query, w_key, w_value)]

        def mix(m, row_block, projected, previous, deps):
            return attend(*projected, row_block, pieces[m], w_out[0].reshape(heads_width, dim), m, micro_count, seq_len, w_query.shape[3], previous, deps)

        here[0] = own(0, (shared[0],))
        last = finish(0, 1, finish(0, 0, (here[0][0],)))
        hidden = hidden_half(1, last)
        here[1] = own(1, (hidden,))
        last = finish(1, 0, (here[1][0],))
        shared.append(down_product(hidden, w_down[0], last))
        last = finish(1, 1, (shared[1],))
        here[2] = own(2, last)
        here[3] = own(3, (here[2][0],))
        both = project((0, 1), (here[3][0],))
        last = finish(2, 1, finish(2, 0, tuple(both)))
        out = mix(0, 0, both, None, last)
        out = mix(1, 1, both, out, ())
        last = finish(3, 1, finish(3, 0, (out,)))
        third = project((2,), last)
        last = finish(3, 2, tuple(third))
        out = mix(2, 0, third, out, last)
        fourth = project((3,), (out,))
        out = mix(3, 0, fourth, out, ())
        return out.reshape(residual.shape)

    in_specs = (tok_spec,) * 5 + (vec_spec, mat_spec, mat_spec, mat_spec, vec_spec, head_spec, head_spec, head_spec, head_spec)

    return jax.shard_map(device_step, mesh=mesh, in_specs=in_specs, out_specs=tok_spec, check_vma=False)
```

time: 1820 us -> 878 us (0.48)
  waiting for transfers between devices: 656 us -> 123 us
  Pallas kernels: 0 us -> 471 us
  local copies, waits for them, and re-layouts: 459 us -> 17.9 us
  matrix products: 542 us -> 227 us
  other arithmetic: 114 us -> 3.27 us
    all_to_all x4 -> x0, waiting for transfers between devices: 656 us -> none  [device_step(): received = lax.all_to_all(local_out, 'ep', 1, 0, tiled=True)]
    pallas_call x0 -> x33, Pallas kernels: none -> 471 us  [the longest x8 112 us: chip_partial(): pl.pallas_call(body, out_shape=[jax.ShapeDtypeStruct((parts * ROWS * tile...]
    dot_general x36 -> x9, matrix products: 542 us -> 227 us  [project(): jnp.dot(normed, flat(weight), preferred_element_type=jnp.float32)]
    gather x4 -> x0, local copies, waits for them, and re-layouts: 175 us -> none  [gather_combine(): picked = jnp.take(row_table, row_ids, axis=0, mode='clip')]
    ppermute x4 -> x27, waiting for transfers between devices: 0.01 us -> 123 us  [the longest x9 75.8 us: device_step(): arrived[m].append(lax.ppermute(part, 'ep', chip_pairs))]
    convert_element_type x4 -> x0, local copies, waits for them, and re-layouts: 119 us -> none  [gather_combine(): return jnp.sum(picked.astype(jnp.float32) * weights[..., None], axis=-2)]
    reduce_sum x10 -> x0, other arithmetic: 106 us -> none  [the longest x4 83 us: gather_combine(): return jnp.sum(picked.astype(jnp.float32) * weights[..., None], axis=-2)]
    another operation x4 -> x0, local copies, waits for them, and re-layouts: 83.7 us -> none  [device_step(): expert_out[0, micro_idx]]
  transfers between devices with their start and end apart: 8 -> 27, of which waited for: 3 -> 5; matrix products, arithmetic and copies ran while one was open for 40% -> 21% of each run, Pallas kernels for 0% -> 50%
where the time goes in v1:
time: 878 us; the launch traced here: 868 us
  Pallas kernels  471 us (54%)
  matrix products  227 us (26%)
  waiting for transfers between devices  123 us (14%)
  starting transfers between devices  26 us (3%)
  local copies, waits for them, and re-layouts  17.9 us (2%)
    dot_general x9, matrix products, project(): jnp.dot(normed, flat(weight), preferred_element_type=jnp.float32)  227 us
    pallas_call x8, Pallas kernels, chip_partial(): pl.pallas_call(body, out_shape=[jax.ShapeDtypeStruct((parts * ROWS * tile...  112 us
    pallas_call x4, Pallas kernels, attend(): pl.pallas_call(body, out_shape=jax.ShapeDtypeStruct((micro_count, tokens,...  108 us
    pallas_call x2, Pallas kernels, gated_hidden(): pl.pallas_call(gated, out_shape=jax.ShapeDtypeStruct((rows, width), jnp.b...  96 us
    ppermute x9, waiting for transfers between devices, device_step(): arrived[m].append(lax.ppermute(part, 'ep', chip_pairs))  75.8 us
    pallas_call x2, Pallas kernels, down_product(): pl.pallas_call(down, out_shape=jax.ShapeDtypeStruct((rows, dim), jnp.bflo...  49.8 us
    ppermute x9, waiting for transfers between devices, finish(): pieces[m].append(lax.ppermute(combined, 'pp', shift_pairs))  45.4 us
    pallas_call x9, Pallas kernels, combine_chunk(): pl.pallas_call(body, out_shape=jax.ShapeDtypeStruct((chunk, dim), jnp.bfl...  45.4 us
  transfers between devices with their start and end apart: 27, of which 5 were waited for; matrix products, arithmetic and copies ran while one was open for 21% of the time, Pallas kernels for 50%

profile of v1, /device:TPU:0, one launch (start us, length us, event | category | flops | bytes accessed | tf_op | source)
XLA Modules:
  0.0 868.3 jit_solution(18270686696824332553)
XLA Ops:
  24.9 13.9 %combine.8 = (f32[6144,128]{1,0:T(8,128)}, f32[6144,128]{1,0:T(8,128)}) custom-call(s32[1]{0:T(128)} %bitcast.6.owner_ref, s32[2304]{0:T(1024)} %get-tuple-element.59.rows_ref, f32[2304]{0:T(1024)} %get-tuple-element.55.gates_ref, bf16[1,4,32,96,4096]{4,3,2,1,0:T(8,128)(2,1)} %own_ref.15, bf16[32,24,4096]{2,1,0:T(8,128)(2,1)} %collective-permute-done.1.sib_ref, ...), custom_call_target="tpu_custom_call" | custom-call | flops 8000000000 | bytes 18874368 | tf_op jit(solution)/shard_map/combine/pallas_call | solution.py:255
  38.8 10.0 %pick.7 = (bf16[32,24,4096]{2,1,0:T(8,128)(2,1)}, bf16[32,24,4096]{2,1,0:T(8,128)(2,1)}) custom-call(s32[2]{0:T(128)} %pad_add_fusion.1.owners_ref, bf16[1,4,32,96,4096]{4,3,2,1,0:T(8,128)(2,1)} %own_ref.15, bf16[1,4,32,96,4096]{4,3,2,1,0:T(8,128)(2,1)} %own_ref.15, f32[6144,128]{1,0:T(8,128)} %get-tuple-element.29.refs_2_), custom_call_target="tpu_custom_call" | custom-call | flops 4000000000 | bytes 25165824 | tf_op jit(solution)/shard_map/pick/pallas_call | solution.py:195
  48.8 13.9 %combine.9 = (f32[6144,128]{1,0:T(8,128)}, f32[6144,128]{1,0:T(8,128)}) custom-call(s32[1]{0:T(128)} %bitcast.6.owner_ref, s32[2304]{0:T(1024)} %get-tuple-element.58.rows_ref, f32[2304]{0:T(1024)} %get-tuple-element.54.gates_ref, bf16[1,4,32,96,4096]{4,3,2,1,0:T(8,128)(2,1)} %own_ref.15, bf16[32,24,4096]{2,1,0:T(8,128)(2,1)} %collective-permute-done.3.sib_ref, ...), custom_call_target="tpu_custom_call" | custom-call | flops 8000000000 | bytes 18874368 | tf_op jit(solution)/shard_map/combine/pallas_call | solution.py:255
  62.7 10.1 %pick.8 = (bf16[32,24,4096]{2,1,0:T(8,128)(2,1)}, bf16[32,24,4096]{2,1,0:T(8,128)(2,1)}) custom-call(s32[2]{0:T(128)} %pad_add_fusion.1.owners_ref, bf16[1,4,32,96,4096]{4,3,2,1,0:T(8,128)(2,1)} %own_ref.15, bf16[1,4,32,96,4096]{4,3,2,1,0:T(8,128)(2,1)} %own_ref.15, f32[6144,128]{1,0:T(8,128)} %get-tuple-element.32.refs_2_), custom_call_target="tpu_custom_call" | custom-call | flops 4000000000 | bytes 25165824 | tf_op jit(solution)/shard_map/pick/pallas_call | solution.py:195
  81.3 13.8 %combine.10 = (f32[6144,128]{1,0:T(8,128)}, f32[6144,128]{1,0:T(8,128)}) custom-call(s32[1]{0:T(128)} %bitcast.6.owner_ref, s32[2304]{0:T(1024)} %get-tuple-element.60.rows_ref, f32[2304]{0:T(1024)} %get-tuple-element.56.gates_ref, bf16[1,4,32,96,4096]{4,3,2,1,0:T(8,128)(2,1)} %own_ref.15, bf16[32,24,4096]{2,1,0:T(8,128)(2,1)} %collective-permute-done.2.sib_ref, ...), custom_call_target="tpu_custom_call" | custom-call | flops 8000000000 | bytes 18874368 | tf_op jit(solution)/shard_map/combine/pallas_call | solution.py:255
  95.2 10.0 %pick.9 = (bf16[32,24,4096]{2,1,0:T(8,128)(2,1)}, bf16[32,24,4096]{2,1,0:T(8,128)(2,1)}) custom-call(s32[2]{0:T(128)} %pad_add_fusion.owners_ref, bf16[1,4,32,96,4096]{4,3,2,1,0:T(8,128)(2,1)} %own_ref.15, bf16[1,4,32,96,4096]{4,3,2,1,0:T(8,128)(2,1)} %own_ref.15, f32[6144,128]{1,0:T(8,128)} %get-tuple-element.34.refs_2_), custom_call_target="tpu_custom_call" | custom-call | flops 4000000000 | bytes 25165824 | tf_op jit(solution)/shard_map/pick/pallas_call | solution.py:195
  107.0 14.4 %combine.11 = (f32[4096,128]{1,0:T(8,128)}, f32[4096,128]{1,0:T(8,128)}, f32[4096,128]{1,0:T(8,128)}) custom-call(s32[1]{0:T(128)} %bitcast.6.owner_ref, s32[2304]{0:T(1024)} %get-tuple-element.57.rows_ref, f32[2304]{0:T(1024)} %get-tuple-element.53.gates_ref, bf16[1,4,32,96,4096]{4,3,2,1,0:T(8,128)(2,1)} %own_ref.15, ...), custom_call_target="tpu_custom_call" | custom-call | flops 8000000000 | bytes 18874368 | tf_op jit(solution)/shard_map/combine/pallas_call | solution.py:255
  121.4 48.0 %gated.2.hidden_ref = bf16[768,2816]{1,0:T(8,128)(2,1)} custom-call(bf16[1536,4096]{1,0:T(8,128)(2,1)} %bitcast.122, f32[1,4096]{1,0:T(1,128)} %gain_ref.3, bf16[4096,2816]{1,0:T(8,128)(2,1)} %bitcast.146, bf16[4096,2816]{1,0:T(8,128)(2,1)} %bitcast.148, f32[4096,128]{1,0:T(8,128)} %get-tuple-element.38.rest_0_), custom_call_target="tpu_custom_call" | custom-call | flops 35433480192 | bytes 46137344 | tf_op jit(solution)/shard_map/gated/pallas_call | solution.py:77
  169.4 25.1 %down.2.rest_0_.sh_ref = bf16[768,4096]{1,0:T(8,128)(2,1)} custom-call(bf16[768,2816]{1,0:T(8,128)(2,1)} %gated.2.hidden_ref, bf16[2816,4096]{1,0:T(8,128)(2,1)} %bitcast.150), custom_call_target="tpu_custom_call" | custom-call | flops 17716740096 | bytes 23068672 | tf_op jit(solution)/shard_map/down/pallas_call | solution.py:111
  194.5 13.8 %combine.12 = (f32[6144,128]{1,0:T(8,128)}, f32[6144,128]{1,0:T(8,128)}) custom-call(s32[1]{0:T(128)} %bitcast.owner_ref, s32[2304]{0:T(1024)} %squeeze.93.rows_ref, f32[2304]{0:T(1024)} %squeeze.94.gates_ref, bf16[1,4,32,96,4096]{4,3,2,1,0:T(8,128)(2,1)} %own_ref.15, bf16[32,24,4096]{2,1,0:T(8,128)(2,1)} %collective-permute-done.7.sib_ref, ...), custom_call_target="tpu_custom_call" | custom-call | flops 8000000000 | bytes 18874368 | tf_op jit(solution)/shard_map/combine/pallas_call | solution.py:255
  214.2 70.6 %collective-permute-done.9.far_ref = f32[6144,128]{1,0:T(8,128)S(1)} collective-permute-done((f32[6144,128]{1,0:T(8,128)}, f32[6144,128]{1,0:T(8,128)S(1)}, u32[]{:S(2)}, u32[]{:S(2)}) %collective-permute-start.9) | collective-permute-done | bytes 3145760 | tf_op jit(solution)/shard_map/ppermute | solution.py:361
  292.1 48.0 %gated.3.rest_0_.hidden_ref = bf16[768,2816]{1,0:T(8,128)(2,1)} custom-call(bf16[1536,4096]{1,0:T(8,128)(2,1)} %bitcast.125, f32[1,4096]{1,0:T(1,128)} %gain_ref.3, bf16[4096,2816]{1,0:T(8,128)(2,1)} %bitcast.147, bf16[4096,2816]{1,0:T(8,128)(2,1)} %bitcast.149, bf16[192,4096]{1,0:T(8,128)(2,1)} %finish.10.rest_0_), custom_call_target="tpu_custom_call" | custom-call | flops 35433480192 | bytes 46137344 | tf_op jit(solution)/shard_map/gated/pallas_call | solution.py:77
  341.9 13.8 %combine.13 = (f32[6144,128]{1,0:T(8,128)}, f32[6144,128]{1,0:T(8,128)}) custom-call(s32[1]{0:T(128)} %bitcast.owner_ref, s32[2304]{0:T(1024)} %squeeze.89.rows_ref, f32[2304]{0:T(1024)} %squeeze.90.gates_ref, bf16[1,4,32,96,4096]{4,3,2,1,0:T(8,128)(2,1)} %own_ref.15, bf16[32,24,4096]{2,1,0:T(8,128)(2,1)} %collective-permute-done.6.sib_ref, ...), custom_call_target="tpu_custom_call" | custom-call | flops 8000000000 | bytes 18874368 | tf_op jit(solution)/shard_map/combine/pallas_call | solution.py:255
  361.7 24.6 %down.3.rest_0_.sh_ref = bf16[768,4096]{1,0:T(8,128)(2,1)} custom-call(bf16[768,2816]{1,0:T(8,128)(2,1)} %gated.3.rest_0_.hidden_ref, bf16[2816,4096]{1,0:T(8,128)(2,1)} %bitcast.151, bf16[192,4096]{1,0:T(8,128)(2,1)} %finish.11.rest_0_), custom_call_target="tpu_custom_call" | custom-call | flops 17716740096 | bytes 23068672 | tf_op jit(solution)/shard_map/down/pallas_call | solution.py:111
  397.6 13.9 %combine.14 = (f32[6144,128]{1,0:T(8,128)}, f32[6144,128]{1,0:T(8,128)}) custom-call(s32[1]{0:T(128)} %bitcast.owner_ref, s32[2304]{0:T(1024)} %squeeze.87.rows_ref, f32[2304]{0:T(1024)} %squeeze.88.gates_ref, bf16[1,4,32,96,4096]{4,3,2,1,0:T(8,128)(2,1)} %own_ref.15, bf16[32,24,4096]{2,1,0:T(8,128)(2,1)} %collective-permute-done.5.sib_ref, ...), custom_call_target="tpu_custom_call" | custom-call | flops 8000000000 | bytes 18874368 | tf_op jit(solution)/shard_map/combine/pallas_call | solution.py:255
  413.2 14.2 %combine.15 = (f32[4096,128]{1,0:T(8,128)}, f32[4096,128]{1,0:T(8,128)}, f32[4096,128]{1,0:T(8,128)}) custom-call(s32[1]{0:T(128)} %bitcast.owner_ref, s32[2304]{0:T(1024)} %squeeze.76.rows_ref, f32[2304]{0:T(1024)} %squeeze.78.gates_ref, bf16[1,4,32,96,4096]{4,3,2,1,0:T(8,128)(2,1)} %own_ref.15, bf16[32,24,4096]{2,1,0:T(8,128)(2,1)} %collective-permute-done.4.sib_ref, ...), custom_call_target="tpu_custom_call" | custom-call | flops 8000000000 | bytes 18874368 | tf_op jit(solution)/shard_map/combine/pallas_call | solution.py:255
  429.5 15.5 %collective-permute-done.16.refs_2_.rest_0_ = bf16[192,4096]{1,0:T(8,128)(2,1)} collective-permute-done((bf16[192,4096]{1,0:T(8,128)(2,1)}, bf16[192,4096]{1,0:T(8,128)(2,1)}, u32[]{:S(2)}, u32[]{:S(2)}) %collective-permute-start.16) | collective-permute-done | bytes 1572896 | tf_op jit(solution)/shard_map/ppermute | solution.py:384
  446.9 29.9 %collective-permute-done.17.refs_3_.rest_1_ = bf16[192,4096]{1,0:T(8,128)(2,1)} collective-permute-done((bf16[192,4096]{1,0:T(8,128)(2,1)}, bf16[192,4096]{1,0:T(8,128)(2,1)}, u32[]{:S(2)}, u32[]{:S(2)}) %collective-permute-start.17) | collective-permute-done | bytes 1572896 | tf_op jit(solution)/shard_map/ppermute | solution.py:384
  478.5 8.0 normalize.3
  486.4 33.4 %fusion.33.rest_2_.v_ref = bf16[768,4096]{1,0:T(8,128)(2,1)} fusion(bf16[768,4096]{1,0:T(8,128)(2,1)} %normalize.3, bf16[512,8,32,128]{3,2,1,0:T(8,128)(2,1)} %bitcast.137), kind=kOutput, calls=%fused_computation.29 | convolution fusion | flops 25772949504 | bytes 46137344 | tf_op jit(solution)/shard_map/dot_general | solution.py:389
  519.9 31.6 %fusion.30.rest_1_.k_ref = bf16[768,4096]{1,0:T(8,128)(2,1)} fusion(bf16[768,4096]{1,0:T(8,128)(2,1)S(1)} %copy-done.1, bf16[512,8,32,128]{3,2,1,0:T(8,128)(2,1)} %bitcast.140), kind=kOutput, calls=%fused_computation.28 | convolution fusion | flops 25772949504 | bytes 46137344 | tf_op jit(solution)/shard_map/dot_general | solution.py:389
  551.5 31.4 %fusion.27.rest_0_.q_ref = bf16[768,4096]{1,0:T(8,128)(2,1)} fusion(bf16[768,4096]{1,0:T(8,128)(2,1)S(1)} %copy-done.1, bf16[512,8,32,128]{3,2,1,0:T(8,128)(2,1)} %bitcast.143), kind=kOutput, calls=%fused_computation.27 | convolution fusion | flops 25772949504 | bytes 46137344 | tf_op jit(solution)/shard_map/dot_general | solution.py:389
  602.5 27.1 %attend.4.rest_2_ = bf16[4,384,4096]{2,1,0:T(8,128)(2,1)} custom-call(bf16[768,4096]{1,0:T(8,128)(2,1)} %fusion.27.rest_0_.q_ref, bf16[768,4096]{1,0:T(8,128)(2,1)} %fusion.30.rest_1_.k_ref, bf16[768,4096]{1,0:T(8,128)(2,1)} %fusion.33.rest_2_.v_ref, bf16[4096,4096]{1,0:T(8,128)(2,1)} %bitcast.133, ...), custom_call_target="tpu_custom_call" | custom-call | flops 12884901888 | bytes 33554432 | tf_op jit(solution)/shard_map/attend/pallas_call | solution.py:168
  629.6 27.0 %attend.5.rest_0_.rest_3_ = bf16[4,384,4096]{2,1,0:T(8,128)(2,1)} custom-call(bf16[768,4096]{1,0:T(8,128)(2,1)} %fusion.27.rest_0_.q_ref, bf16[768,4096]{1,0:T(8,128)(2,1)} %fusion.30.rest_1_.k_ref, bf16[768,4096]{1,0:T(8,128)(2,1)} %fusion.33.rest_2_.v_ref, bf16[4096,4096]{1,0:T(8,128)(2,1)} %bitcast.134, ...), custom_call_target="tpu_custom_call", output_to_operand_aliasing={{}: (6, {})} | custom-call | flops 12884901888 | bytes 33554432 | tf_op jit(solution)/shard_map/attend/pallas_call | solution.py:168
  673.6 26.3 %fusion.48.rest_2_.v_ref = bf16[384,4096]{1,0:T(8,128)(2,1)} fusion(bf16[384,4096]{1,0:T(8,128)(2,1)} %normalize.4, bf16[512,8,32,128]{3,2,1,0:T(8,128)(2,1)} %bitcast.138), kind=kOutput, calls=%fused_computation.34 | convolution fusion | flops 12886474752 | bytes 39845888 | tf_op jit(solution)/shard_map/dot_general | solution.py:389
  699.9 20.5 %fusion.42.rest_1_.k_ref = bf16[384,4096]{1,0:T(8,128)(2,1)} fusion(bf16[384,4096]{1,0:T(8,128)(2,1)S(1)} %copy-done.7, bf16[512,8,32,128]{3,2,1,0:T(8,128)(2,1)} %bitcast.141), kind=kOutput, calls=%fused_computation.32 | convolution fusion | flops 12886474752 | bytes 39845888 | tf_op jit(solution)/shard_map/dot_general | solution.py:389
  720.5 20.6 %fusion.36.rest_0_.q_ref = bf16[384,4096]{1,0:T(8,128)(2,1)} fusion(bf16[384,4096]{1,0:T(8,128)(2,1)S(1)} %copy-done.7, bf16[512,8,32,128]{3,2,1,0:T(8,128)(2,1)} %bitcast.144), kind=kOutput, calls=%fused_computation.30 | convolution fusion | flops 12886474752 | bytes 39845888 | tf_op jit(solution)/shard_map/dot_general | solution.py:389
  745.2 26.9 %attend.6.refs_4_.rest_3_ = bf16[4,384,4096]{2,1,0:T(8,128)(2,1)} custom-call(bf16[384,4096]{1,0:T(8,128)(2,1)} %fusion.36.rest_0_.q_ref, bf16[384,4096]{1,0:T(8,128)(2,1)} %fusion.42.rest_1_.k_ref, bf16[384,4096]{1,0:T(8,128)(2,1)} %fusion.48.rest_2_.v_ref, bf16[4096,4096]{1,0:T(8,128)(2,1)} %bitcast.135, ...), custom_call_target="tpu_custom_call", output_to_operand_aliasing={{}: (7, {})} | custom-call | flops 12884901888 | bytes 33554432 | tf_op jit(solution)/shard_map/attend/pallas_call | solution.py:168
  778.4 21.5 %fusion.51.v_ref = bf16[384,4096]{1,0:T(8,128)(2,1)} fusion(bf16[384,4096]{1,0:T(8,128)(2,1)} %normalize.5, bf16[512,8,32,128]{3,2,1,0:T(8,128)(2,1)} %bitcast.139), kind=kOutput, calls=%fused_computation.35 | convolution fusion | flops 12886474752 | bytes 39845888 | tf_op jit(solution)/shard_map/dot_general | solution.py:389
  799.8 20.8 %fusion.45.k_ref = bf16[384,4096]{1,0:T(8,128)(2,1)} fusion(bf16[384,4096]{1,0:T(8,128)(2,1)S(1)} %copy-done.8, bf16[512,8,32,128]{3,2,1,0:T(8,128)(2,1)} %bitcast.142), kind=kOutput, calls=%fused_computation.33 | convolution fusion | flops 12886474752 | bytes 39845888 | tf_op jit(solution)/shard_map/dot_general | solution.py:389
  820.7 20.6 %fusion.39.q_ref = bf16[384,4096]{1,0:T(8,128)(2,1)} fusion(bf16[384,4096]{1,0:T(8,128)(2,1)S(1)} %copy-done.8, bf16[512,8,32,128]{3,2,1,0:T(8,128)(2,1)} %bitcast.145), kind=kOutput, calls=%fused_computation.31 | convolution fusion | flops 12886474752 | bytes 39845888 | tf_op jit(solution)/shard_map/dot_general | solution.py:389
  841.3 26.9 %attend.7 = bf16[4,384,4096]{2,1,0:T(8,128)(2,1)} custom-call(bf16[384,4096]{1,0:T(8,128)(2,1)} %fusion.39.q_ref, bf16[384,4096]{1,0:T(8,128)(2,1)} %fusion.45.k_ref, bf16[384,4096]{1,0:T(8,128)(2,1)} %fusion.51.v_ref, bf16[4096,4096]{1,0:T(8,128)(2,1)} %bitcast.136, ...), custom_call_target="tpu_custom_call", output_to_operand_aliasing={{}: (7, {})} | custom-call | flops 12884901888 | bytes 33554432 | tf_op jit(solution)/shard_map/attend/pallas_call | solution.py:168
  (136 shorter events, 121.7 us)
Async XLA Ops:
  5.9 19.0 %collective-permute-start.1 = (bf16[32,24,4096]{2,1,0:T(8,128)(2,1)}, bf16[32,24,4096]{2,1,0:T(8,128)(2,1)}, u32[]{:S(2)}, u32[]{:S(2)}) collective-permute-start(bf16[32,24,4096]{2,1,0:T(8,128)(2,1)} %pick.5.refs_1_), channel_id=1, source_target_pairs={{0,1},{1,0},{2,3},{3,2},{4,5},{5,4},{6,7},{7,6}} | collective-permute-start | bytes 18874376 | tf_op jit(solution)/shard_map/ppermute | solution.py:351
  12.8 36.0 %collective-permute-start.3 = (bf16[32,24,4096]{2,1,0:T(8,128)(2,1)}, bf16[32,24,4096]{2,1,0:T(8,128)(2,1)}, u32[]{:S(2)}, u32[]{:S(2)}) collective-permute-start(bf16[32,24,4096]{2,1,0:T(8,128)(2,1)} %pick.6.rest_0_), channel_id=1, source_target_pairs={{0,1},{1,0},{2,3},{3,2},{4,5},{5,4},{6,7},{7,6}} | collective-permute-start | bytes 18874376 | tf_op jit(solution)/shard_map/ppermute | solution.py:351
  18.1 5.4 collective-permute-start
  48.8 32.0 %collective-permute-start.2 = (bf16[32,24,4096]{2,1,0:T(8,128)(2,1)}, bf16[32,24,4096]{2,1,0:T(8,128)(2,1)}, u32[]{:S(2)}, u32[]{:S(2)}) collective-permute-start(bf16[32,24,4096]{2,1,0:T(8,128)(2,1)} %get-tuple-element.30), channel_id=1, source_target_pairs={{0,1},{1,0},{2,3},{3,2},{4,5},{5,4},{6,7},{7,6}} | collective-permute-start | bytes 18874376 | tf_op jit(solution)/shard_map/ppermute | solution.py:351
  72.8 32.4 %collective-permute-start.8 = (bf16[32,24,4096]{2,1,0:T(8,128)(2,1)}, bf16[32,24,4096]{2,1,0:T(8,128)(2,1)}, u32[]{:S(2)}, u32[]{:S(2)}) collective-permute-start(bf16[32,24,4096]{2,1,0:T(8,128)(2,1)} %get-tuple-element.37), channel_id=1, source_target_pairs={{0,1},{1,0},{2,3},{3,2},{4,5},{5,4},{6,7},{7,6}} | collective-permute-start | bytes 18874376 | tf_op jit(solution)/shard_map/ppermute | solution.py:351
  78.8 129.6 %collective-permute-start.10 = (f32[6144,128]{1,0:T(8,128)}, f32[6144,128]{1,0:T(8,128)}, u32[]{:S(2)}, u32[]{:S(2)}) collective-permute-start(f32[6144,128]{1,0:T(8,128)} %get-tuple-element.29.refs_2_), channel_id=1, source_target_pairs={{0,2},{1,3},{2,0},{3,1},{4,6},{5,7},{6,4},{7,5}} | collective-permute-start | bytes 9437192 | tf_op jit(solution)/shard_map/ppermute | solution.py:361
  80.6 275.1 %collective-permute-start.12 = (f32[6144,128]{1,0:T(8,128)}, f32[6144,128]{1,0:T(8,128)}, u32[]{:S(2)}, u32[]{:S(2)}) collective-permute-start(f32[6144,128]{1,0:T(8,128)} %get-tuple-element.32.refs_2_), channel_id=1, source_target_pairs={{0,2},{1,3},{2,0},{3,1},{4,6},{5,7},{6,4},{7,5}} | collective-permute-start | bytes 9437192 | tf_op jit(solution)/shard_map/ppermute | solution.py:361
  80.8 113.7 %collective-permute-start.7 = (bf16[32,24,4096]{2,1,0:T(8,128)(2,1)}, bf16[32,24,4096]{2,1,0:T(8,128)(2,1)}, u32[]{:S(2)}, u32[]{:S(2)}) collective-permute-start(bf16[32,24,4096]{2,1,0:T(8,128)(2,1)} %get-tuple-element.31.rest_0_), channel_id=1, source_target_pairs={{0,1},{1,0},{2,3},{3,2},{4,5},{5,4},{6,7},{7,6}} | collective-permute-start | bytes 18874376 | tf_op jit(solution)/shard_map/ppermute | solution.py:351
  80.8 259.2 %collective-permute-start.6 = (bf16[32,24,4096]{2,1,0:T(8,128)(2,1)}, bf16[32,24,4096]{2,1,0:T(8,128)(2,1)}, u32[]{:S(2)}, u32[]{:S(2)}) collective-permute-start(bf16[32,24,4096]{2,1,0:T(8,128)(2,1)} %get-tuple-element.33.rest_0_), channel_id=1, source_target_pairs={{0,1},{1,0},{2,3},{3,2},{4,5},{5,4},{6,7},{7,6}} | collective-permute-start | bytes 18874376 | tf_op jit(solution)/shard_map/ppermute | solution.py:351
  105.2 179.6 %collective-permute-start.9 = (f32[6144,128]{1,0:T(8,128)}, f32[6144,128]{1,0:T(8,128)S(1)}, u32[]{:S(2)}, u32[]{:S(2)}) collective-permute-start(f32[6144,128]{1,0:T(8,128)} %get-tuple-element.40), channel_id=1, source_target_pairs={{0,2},{1,3},{2,0},{3,1},{4,6},{5,7},{6,4},{7,5}} | collective-permute-start | bytes 9437192 | tf_op jit(solution)/shard_map/ppermute | solution.py:361
  194.5 199.2 %collective-permute-start.5 = (bf16[32,24,4096]{2,1,0:T(8,128)(2,1)}, bf16[32,24,4096]{2,1,0:T(8,128)(2,1)}, u32[]{:S(2)}, u32[]{:S(2)}) collective-permute-start(bf16[32,24,4096]{2,1,0:T(8,128)(2,1)} %get-tuple-element.36), channel_id=1, source_target_pairs={{0,1},{1,0},{2,3},{3,2},{4,5},{5,4},{6,7},{7,6}} | collective-permute-start | bytes 18874376 | tf_op jit(solution)/shard_map/ppermute | solution.py:351
  208.4 178.0 %collective-permute-start.11 = (f32[6144,128]{1,0:T(8,128)}, f32[6144,128]{1,0:T(8,128)}, u32[]{:S(2)}, u32[]{:S(2)}) collective-permute-start(f32[6144,128]{1,0:T(8,128)} %get-tuple-element.43), channel_id=1, source_target_pairs={{0,2},{1,3},{2,0},{3,1},{4,6},{5,7},{6,4},{7,5}} | collective-permute-start | bytes 9437192 | tf_op jit(solution)/shard_map/ppermute | solution.py:361
  284.8 126.7 %collective-permute-start.4 = (bf16[32,24,4096]{2,1,0:T(8,128)(2,1)}, bf16[32,24,4096]{2,1,0:T(8,128)(2,1)}, u32[]{:S(2)}, u32[]{:S(2)}) collective-permute-start(bf16[32,24,4096]{2,1,0:T(8,128)(2,1)} %get-tuple-element.35.rest_0_), channel_id=1, source_target_pairs={{0,1},{1,0},{2,3},{3,2},{4,5},{5,4},{6,7},{7,6}} | collective-permute-start | bytes 18874376 | tf_op jit(solution)/shard_map/ppermute | solution.py:351
  340.0 15.7 %copy-start = (bf16[192,4096]{1,0:T(8,128)(2,1)S(1)}, bf16[192,4096]{1,0:T(8,128)(2,1)}, u32[]{:S(2)}) copy-start(bf16[192,4096]{1,0:T(8,128)(2,1)} %finish.9.rest_0_) | copy-start | bytes 4718596
  340.0 87.4 %collective-permute-start.15 = (bf16[192,4096]{1,0:T(8,128)(2,1)}, bf16[192,4096]{1,0:T(8,128)(2,1)S(1)}, u32[]{:S(2)}, u32[]{:S(2)}) collective-permute-start(bf16[192,4096]{1,0:T(8,128)(2,1)} %finish.10.rest_0_), channel_id=1, source_target_pairs={{0,4},{4,0},{1,5},{5,1},{2,6},{6,2},{3,7},{7,3}} | collective-permute-start | bytes 4718600 | tf_op jit(solution)/shard_map/ppermute | solution.py:384
  355.8 72.0 %collective-permute-start.14 = (bf16[192,4096]{1,0:T(8,128)(2,1)S(1)}, bf16[192,4096]{1,0:T(8,128)(2,1)}, u32[]{:S(2)}, u32[]{:S(2)}) collective-permute-start(bf16[192,4096]{1,0:T(8,128)(2,1)S(1)} %copy-done), channel_id=1, source_target_pairs={{0,4},{4,0},{1,5},{5,1},{2,6},{6,2},{3,7},{7,3}} | collective-permute-start | bytes 4718600 | tf_op jit(solution)/shard_map/ppermute | solution.py:384
  386.3 58.7 %collective-permute-start.16 = (bf16[192,4096]{1,0:T(8,128)(2,1)}, bf16[192,4096]{1,0:T(8,128)(2,1)}, u32[]{:S(2)}, u32[]{:S(2)}) collective-permute-start(bf16[192,4096]{1,0:T(8,128)(2,1)} %finish.11.rest_0_), channel_id=1, source_target_pairs={{0,4},{4,0},{1,5},{5,1},{2,6},{6,2},{3,7},{7,3}} | collective-permute-start | bytes 4718600 | tf_op jit(solution)/shard_map/ppermute | solution.py:384
  393.7 83.0 %collective-permute-start.17 = (bf16[192,4096]{1,0:T(8,128)(2,1)}, bf16[192,4096]{1,0:T(8,128)(2,1)}, u32[]{:S(2)}, u32[]{:S(2)}) collective-permute-start(bf16[192,4096]{1,0:T(8,128)(2,1)} %finish.12.rest_0_), channel_id=1, source_target_pairs={{0,4},{4,0},{1,5},{5,1},{2,6},{6,2},{3,7},{7,3}} | collective-permute-start | bytes 4718600 | tf_op jit(solution)/shard_map/ppermute | solution.py:384
  411.5 171.3 %collective-permute-start.19 = (f32[6144,128]{1,0:T(8,128)}, f32[6144,128]{1,0:T(8,128)}, u32[]{:S(2)}, u32[]{:S(2)}) collective-permute-start(f32[6144,128]{1,0:T(8,128)} %get-tuple-element.34.refs_2_), channel_id=1, source_target_pairs={{0,2},{1,3},{2,0},{3,1},{4,6},{5,7},{6,4},{7,5}} | collective-permute-start | bytes 9437192 | tf_op jit(solution)/shard_map/ppermute | solution.py:361
  427.5 51.0 %copy-start.4 = (bf16[192,4096]{1,0:T(8,128)(2,1)}, bf16[192,4096]{1,0:T(8,128)(2,1)S(1)}, u32[]{:S(2)}) copy-start(bf16[192,4096]{1,0:T(8,128)(2,1)S(1)} %collective-permute-done.15.refs_1_.rest_1_) | copy-start | bytes 4718596
  427.5 229.1 %collective-permute-start.13 = (f32[4096,128]{1,0:T(8,128)}, f32[4096,128]{1,0:T(8,128)}, u32[]{:S(2)}, u32[]{:S(2)}) collective-permute-start(f32[4096,128]{1,0:T(8,128)} %get-tuple-element.38.rest_0_), channel_id=1, source_target_pairs={{0,2},{1,3},{2,0},{3,1},{4,6},{5,7},{6,4},{7,5}} | collective-permute-start | bytes 6291464 | tf_op jit(solution)/shard_map/ppermute | solution.py:361
  427.8 167.3 %collective-permute-start.18 = (f32[6144,128]{1,0:T(8,128)}, f32[6144,128]{1,0:T(8,128)}, u32[]{:S(2)}, u32[]{:S(2)}) collective-permute-start(f32[6144,128]{1,0:T(8,128)} %get-tuple-element.48), channel_id=1, source_target_pairs={{0,2},{1,3},{2,0},{3,1},{4,6},{5,7},{6,4},{7,5}} | collective-permute-start | bytes 9437192 | tf_op jit(solution)/shard_map/ppermute | solution.py:361
  445.0 215.7 %collective-permute-start.21 = (f32[4096,128]{1,0:T(8,128)}, f32[4096,128]{1,0:T(8,128)}, u32[]{:S(2)}, u32[]{:S(2)}) collective-permute-start(f32[4096,128]{1,0:T(8,128)} %get-tuple-element.50), channel_id=1, source_target_pairs={{0,2},{1,3},{2,0},{3,1},{4,6},{5,7},{6,4},{7,5}} | collective-permute-start | bytes 6291464 | tf_op jit(solution)/shard_map/ppermute | solution.py:361
  476.8 264.3 %collective-permute-start.23 = (f32[4096,128]{1,0:T(8,128)}, f32[4096,128]{1,0:T(8,128)}, u32[]{:S(2)}, u32[]{:S(2)}) collective-permute-start(f32[4096,128]{1,0:T(8,128)} %get-tuple-element.52), channel_id=1, source_target_pairs={{0,2},{1,3},{2,0},{3,1},{4,6},{5,7},{6,4},{7,5}} | collective-permute-start | bytes 6291464 | tf_op jit(solution)/shard_map/ppermute | solution.py:361
  486.4 33.4 %copy-start.1 = (bf16[768,4096]{1,0:T(8,128)(2,1)S(1)}, bf16[768,4096]{1,0:T(8,128)(2,1)}, u32[]{:S(2)}) copy-start(bf16[768,4096]{1,0:T(8,128)(2,1)} %normalize.3) | copy-start | bytes 18874372
  588.5 77.9 %collective-permute-start.24 = (bf16[192,4096]{1,0:T(8,128)(2,1)}, bf16[192,4096]{1,0:T(8,128)(2,1)S(1)}, u32[]{:S(2)}, u32[]{:S(2)}) collective-permute-start(bf16[192,4096]{1,0:T(8,128)(2,1)} %finish.13.rest_0_), channel_id=1, source_target_pairs={{0,4},{4,0},{1,5},{5,1},{2,6},{6,2},{3,7},{7,3}} | collective-permute-start | bytes 4718600 | tf_op jit(solution)/shard_map/ppermute | solution.py:384
  600.8 65.6 %collective-permute-start.25 = (bf16[192,4096]{1,0:T(8,128)(2,1)}, bf16[192,4096]{1,0:T(8,128)(2,1)S(1)}, u32[]{:S(2)}, u32[]{:S(2)}) collective-permute-start(bf16[192,4096]{1,0:T(8,128)(2,1)} %finish.14.rest_2_), channel_id=1, source_target_pairs={{0,4},{4,0},{1,5},{5,1},{2,6},{6,2},{3,7},{7,3}} | collective-permute-start | bytes 4718600 | tf_op jit(solution)/shard_map/ppermute | solution.py:384
  660.5 111.6 %collective-permute-start.20 = (bf16[128,4096]{1,0:T(8,128)(2,1)}, bf16[128,4096]{1,0:T(8,128)(2,1)}, u32[]{:S(2)}, u32[]{:S(2)}) collective-permute-start(bf16[128,4096]{1,0:T(8,128)(2,1)} %finish.15.rest_0_), channel_id=1, source_target_pairs={{0,4},{4,0},{1,5},{5,1},{2,6},{6,2},{3,7},{7,3}} | collective-permute-start | bytes 3145736 | tf_op jit(solution)/shard_map/ppermute | solution.py:384
  664.6 107.5 %collective-permute-start.22 = (bf16[128,4096]{1,0:T(8,128)(2,1)}, bf16[128,4096]{1,0:T(8,128)(2,1)}, u32[]{:S(2)}, u32[]{:S(2)}) collective-permute-start(bf16[128,4096]{1,0:T(8,128)(2,1)} %finish.16.refs_3_), channel_id=1, source_target_pairs={{0,4},{4,0},{1,5},{5,1},{2,6},{6,2},{3,7},{7,3}} | collective-permute-start | bytes 3145736 | tf_op jit(solution)/shard_map/ppermute | solution.py:384
  673.6 26.4 %copy-start.7 = (bf16[384,4096]{1,0:T(8,128)(2,1)S(1)}, bf16[384,4096]{1,0:T(8,128)(2,1)}, u32[]{:S(2)}) copy-start(bf16[384,4096]{1,0:T(8,128)(2,1)} %normalize.4) | copy-start | bytes 9437188
  744.9 27.2 %collective-permute-start.26 = (bf16[128,4096]{1,0:T(8,128)(2,1)}, bf16[128,4096]{1,0:T(8,128)(2,1)S(1)}, u32[]{:S(2)}, u32[]{:S(2)}) collective-permute-start(bf16[128,4096]{1,0:T(8,128)(2,1)} %finish.17.rest_2_), channel_id=1, source_target_pairs={{0,4},{4,0},{1,5},{5,1},{2,6},{6,2},{3,7},{7,3}} | collective-permute-start | bytes 3145736 | tf_op jit(solution)/shard_map/ppermute | solution.py:384
  778.4 21.5 %copy-start.8 = (bf16[384,4096]{1,0:T(8,128)(2,1)S(1)}, bf16[384,4096]{1,0:T(8,128)(2,1)}, u32[]{:S(2)}) copy-start(bf16[384,4096]{1,0:T(8,128)(2,1)} %normalize.5) | copy-start | bytes 9437188
  (13 other events, 78.6 us)

commit v2 on v1

--- a/solution.py
+++ b/solution.py
@@ -8,7 +8,7 @@
 
 EPSILON = 1e-6
 LANES = 128
-CHUNKS = (2, 2, 2, 3)
+CHUNKS = (1, 3, 2, 3)
 ROWS = 64
 VMEM_LIMIT = 60 << 20
 ANY = pl.BlockSpec(memory_space=pl.ANY)
@@ -16,7 +16,7 @@
 
 def normalize(blocks, gain, deps=()):
     dim = blocks[0].shape[1]
-    step = blocks[0].shape[0]
+    step = math.gcd(*[block.shape[0] for block in blocks])
     counts = [block.shape[0] // step for block in blocks]
     starts = [sum(counts[:c]) for c in range(len(blocks))]
     total = sum(counts)
@@ -48,7 +48,7 @@
 def gated_hidden(residual, part, parts, gain, w_gate, w_up, deps=()):
     rows, dim = residual.shape[0] // parts, residual.shape[1]
     width = w_gate.shape[1]
-    block = 384
+    block = 768
     cols = 256
 
     def gated(res_ref, gain_ref, gate_ref, up_ref, *rest):
@@ -95,7 +95,7 @@
 def down_product(hidden, w_down, deps=()):
     rows, width = hidden.shape
     dim = w_down.shape[1]
-    block = 384
+    block = 768
     out_cols = 512
 
     def down(hidden_ref, w_ref, *rest):
@@ -127,7 +127,7 @@
     width = queries.shape[1]
     dim = w_out.shape[1]
     cols = 1024
-    group = 4
+    group = 8
     pair = 2 * seq_len
     core_steps = width // (group * head_dim)
     scale = 1.0 / math.sqrt(head_dim)
@@ -182,7 +182,7 @@
 
 def pick_rows(expert_out, picks, cap, deps=()):
     experts, _, dim = expert_out.shape[2:]
-    step = 8
+    step = 16
     count = len(picks)
 
     def body(owners_ref, *refs):
@@ -208,74 +208,77 @@
 
 def chip_partial(expert_out, sibling_rows, micro, owner, rows, gates, tokens, top_k, chunks, deps=()):
     experts, cap, dim = sibling_rows.shape
-    step = 16
+    step = 4
+    streams = 2
     tiles = dim // LANES
-    half = experts // step
+    steps = experts // (step * streams)
     pitch = 2 * experts * cap + 1
-    parts = tokens // chunks // ROWS
-
-    def body(owner_ref, rows_ref, gates_ref, own_ref, sib_ref, *rest):
-        outs, table = rest[len(deps):-1], rest[-1]
+    count = min(128, tokens // chunks)
+    while (tokens // chunks) % count:
+        count -= 32
+    parts = tokens // chunks // count
+
+    def body(owner_ref, rows_ref, gates_ref, *rest):
+        sources = rest[:2 * streams]
+        outs, table = rest[2 * streams + len(deps):-1], rest[-1]
         s = pl.program_id(0)
 
-        def put(ref, base):
-            for e in range(step):
-                for j in range(tiles):
-                    table[pl.ds(j * pitch + base + e * cap, cap), :] = ref[e, :, j * LANES:(j + 1) * LANES].astype(jnp.float32)
-
-        base = pl.multiple_of(s * (step * cap), 8)
-
-        @pl.when(s < half)
+        @pl.when(s < steps)
         def _():
-            put(own_ref.at[0, 0], base)
-
-        @pl.when((s >= half) & (s < 2 * half))
-        def _():
-            put(sib_ref, base)
+            for k, ref in enumerate(sources):
+                base = pl.multiple_of((k * steps + s) * (step * cap), 8)
+                for e in range(step):
+                    for j in range(tiles):
+                        rows_e = ref[0, 0, e, :, j * LANES:(j + 1) * LANES] if k < streams else ref[e, :, j * LANES:(j + 1) * LANES]
+                        table[pl.ds(j * pitch + base + e * cap, cap), :] = rows_e.astype(jnp.float32)
 
         for c, out_ref in enumerate(outs):
-            first = 2 * half + c * parts
+            first = steps + c * parts
 
             @pl.when((s >= first) & (s < first + parts))
             def _():
                 def token(t, carry):
                     acc = None
                     for j in range(top_k):
-                        at = ((s - 2 * half) * ROWS + t) * top_k + j
+                        at = ((s - steps) * count + t) * top_k + j
                         term = table[pl.ds(rows_ref[at], tiles, stride=pitch), :] * gates_ref[at]
                         acc = term if acc is None else acc + term
                     out_ref[pl.ds(pl.multiple_of(t * tiles, tiles), tiles), :] = acc
                     return carry
 
-                lax.fori_loop(0, ROWS, token, 0, unroll=4)
+                lax.fori_loop(0, count, token, 0, unroll=8)
+
+    def own_spec(k):
+        return pl.BlockSpec((1, 1, step, cap, dim), lambda s, o, r, g: (0, micro, k * steps + jnp.minimum(s, steps - 1), o[0], 0))
+
+    def sibling_spec(k):
+        return pl.BlockSpec((step, cap, dim), lambda s, o, r, g: (k * steps + jnp.minimum(s, steps - 1), 0, 0))
 
     def out_spec(c):
-        return pl.BlockSpec((ROWS * tiles, LANES), lambda s, o, r, g: (jnp.clip(s - 2 * half - c * parts, 0, parts - 1), 0))
+        return pl.BlockSpec((count * tiles, LANES), lambda s, o, r, g: (jnp.clip(s - steps - c * parts, 0, parts - 1), 0))
 
     return pl.pallas_call(
         body,
-        out_shape=[jax.ShapeDtypeStruct((parts * ROWS * tiles, LANES), jnp.float32)] * chunks,
+        out_shape=[jax.ShapeDtypeStruct((parts * count * tiles, LANES), jnp.float32)] * chunks,
         grid_spec=pltpu.PrefetchScalarGridSpec(
             num_scalar_prefetch=3,
-            grid=(2 * half + chunks * parts,),
-            in_specs=[
-                pl.BlockSpec((1, 1, step, cap, dim), lambda s, o, r, g: (0, micro, jnp.minimum(s, half - 1), o[0], 0)),
-                pl.BlockSpec((step, cap, dim), lambda s, o, r, g: (jnp.clip(s - half, 0, half - 1), 0, 0)),
-            ] + [ANY] * len(deps),
+            grid=(steps + chunks * parts,),
+            in_specs=[own_spec(k) for k in range(streams)] + [sibling_spec(k) for k in range(streams)] + [ANY] * len(deps),
             out_specs=[out_spec(c) for c in range(chunks)],
             scratch_shapes=[pltpu.VMEM((tiles * pitch, LANES), jnp.float32)],
         ),
         compiler_params=pltpu.CompilerParams(vmem_limit_bytes=VMEM_LIMIT),
         cost_estimate=pl.CostEstimate(flops=8_000_000_000, bytes_accessed=3 * experts * cap * dim * 2, transcendentals=0),
         name="combine",
-    )(owner, rows, gates, expert_out, sibling_rows, *deps)
+    )(owner, rows, gates, *([expert_out] * streams), *([sibling_rows] * streams), *deps)
 
 
 def combine_chunk(own_part, far_part, residual, shared, start, sh_start, deps=()):
     dim = residual.shape[1]
     tiles = dim // LANES
     chunk = own_part.shape[0] // tiles
-    pitch = ROWS + 2
+    block = 96 if chunk % 96 == 0 else ROWS
+    pitch = block + 2
 
     def body(own_ref, far_ref, res_ref, sh_ref, *rest):
         out_ref, planes = rest[-2:]
@@ -285,20 +288,20 @@
             planes[pl.ds(t, tiles, stride=pitch), :] = own_ref[at, :] + far_ref[at, :]
             return carry
 
-        lax.fori_loop(0, ROWS, token, 0, unroll=8)
+        lax.fori_loop(0, block, token, 0, unroll=8)
         for j in range(tiles):
             at = slice(j * LANES, (j + 1) * LANES)
-            total = res_ref[:, at].astype(jnp.float32) + sh_ref[:, at].astype(jnp.float32) + planes[j * pitch:j * pitch + ROWS, :]
+            total = res_ref[:, at].astype(jnp.float32) + sh_ref[:, at].astype(jnp.float32) + planes[j * pitch:j * pitch + block, :]
             out_ref[:, at] = total.astype(jnp.bfloat16)
 
-    part_spec = pl.BlockSpec((ROWS * tiles, LANES), lambda s: (s, 0))
-    rows_from = lambda first: pl.BlockSpec((ROWS, dim), lambda s: (first // ROWS + s, 0))
+    part_spec = pl.BlockSpec((block * tiles, LANES), lambda s: (s, 0))
+    rows_from = lambda first: pl.BlockSpec((block, dim), lambda s: (first // block + s, 0))
     return pl.pallas_call(
         body,
         out_shape=jax.ShapeDtypeStruct((chunk, dim), jnp.bfloat16),
-        grid=(chunk // ROWS,),
+        grid=(chunk // block,),
         in_specs=[part_spec, part_spec, rows_from(start), rows_from(sh_start)] + [ANY] * len(deps),
-        out_specs=pl.BlockSpec((ROWS, dim), lambda s: (s, 0)),
+        out_specs=pl.BlockSpec((block, dim), lambda s: (s, 0)),
         scratch_shapes=[pltpu.VMEM((tiles * pitch, LANES), jnp.float32)],
         cost_estimate=pl.CostEstimate(flops=1_000_000_000, bytes_accessed=14 * chunk * dim, transcendentals=0),
         name="finish",
@@ -392,21 +395,23 @@
             return attend(*projected, row_block, pieces[m], w_out[0].reshape(heads_width, dim), m, micro_count, seq_len, w_query.shape[3], previous, deps)
 
         here[0] = own(0, (shared[0],))
-        last = finish(0, 1, finish(0, 0, (here[0][0],)))
+        last = finish(0, 0, (here[0][0],))
         hidden = hidden_half(1, last)
         here[1] = own(1, (hidden,))
-        last = finish(1, 0, (here[1][0],))
+        last = finish(1, 1, finish(1, 0, (here[1][0],)))
         shared.append(down_product(hidden, w_down[0], last))
-        last = finish(1, 1, (shared[1],))
-        here[2] = own(2, last)
-        here[3] = own(3, (here[2][0],))
+        here[2] = own(2, (shared[1],))
+        last = finish(1, 2, (here[2][0],))
+        here[3] = own(3, last)
         both = project((0, 1), (here[3][0],))
-        last = finish(2, 1, finish(2, 0, tuple(both)))
+        last = finish(2, 0, (both[2],))
+        last = finish(2, 1, (*both, *last))
         out = mix(0, 0, both, None, last)
         out = mix(1, 1, both, out, ())
-        last = finish(3, 1, finish(3, 0, (out,)))
+        last = finish(3, 0, (out,))
         third = project((2,), last)
-        last = finish(3, 2, tuple(third))
+        last = finish(3, 1, (third[2],))
+        last = finish(3, 2, (third[1], *last))
         out = mix(2, 0, third, out, last)
         fourth = project((3,), (out,))
         out = mix(3, 0, fourth, out, ())

time: 878 us -> 809 us (0.921)
  waiting for transfers between devices: 123 us -> 85.6 us
  Pallas kernels: 471 us -> 442 us
    ppermute x9, waiting for transfers between devices: 75.8 us -> 34.6 us  [device_step(): arrived[m].append(lax.ppermute(part, 'ep', chip_pairs))]
  transfers between devices with their start and end apart: 27 -> 27, of which waited for: 5 -> 8; matrix products, arithmetic and copies ran while one was open for 21% -> 23% of each run, Pallas kernels for 50% -> 51%
where the time goes in v2:
time: 809 us; the launch traced here: 801 us
  Pallas kernels  442 us (55%)
  matrix products  228 us (28%)
  waiting for transfers between devices  85.6 us (11%)
  starting transfers between devices  25.5 us (3%)
  local copies, waits for them, and re-layouts  16.9 us (2%)
    dot_general x9, matrix products, project(): jnp.dot(normed, flat(weight), preferred_element_type=jnp.float32)  228 us
    pallas_call x8, Pallas kernels, chip_partial(): pl.pallas_call(body, out_shape=[jax.ShapeDtypeStruct((parts * count * til...  103 us
    pallas_call x4, Pallas kernels, attend(): pl.pallas_call(body, out_shape=jax.ShapeDtypeStruct((micro_count, tokens,...  101 us
    pallas_call x2, Pallas kernels, gated_hidden(): pl.pallas_call(gated, out_shape=jax.ShapeDtypeStruct((rows, width), jnp.b...  92.5 us
    ppermute x9, waiting for transfers between devices, finish(): pieces[m].append(lax.ppermute(combined, 'pp', shift_pairs))  49.1 us
    pallas_call x2, Pallas kernels, down_product(): pl.pallas_call(down, out_shape=jax.ShapeDtypeStruct((rows, dim), jnp.bflo...  46.6 us
    pallas_call x9, Pallas kernels, combine_chunk(): pl.pallas_call(body, out_shape=jax.ShapeDtypeStruct((chunk, dim), jnp.bfl...  42 us
    pallas_call x5, Pallas kernels, pick_rows(): pl.pallas_call(body, out_shape=[jax.ShapeDtypeStruct((experts, cap, dim),...  37.8 us
  transfers between devices with their start and end apart: 27, of which 8 were waited for; matrix products, arithmetic and copies ran while one was open for 23% of the time, Pallas kernels for 51%

profile of v2, /device:TPU:0, one launch (start us, length us, event | category | flops | bytes accessed | tf_op | source)
XLA Modules:
  0.0 801.1 jit_solution(2757946847984995003)
XLA Ops:
  22.6 12.1 %combine.8.refs_2_ = f32[12288,128]{1,0:T(8,128)} custom-call(s32[1]{0:T(128)} %bitcast.6.owner_ref, s32[2304]{0:T(1024)} %get-tuple-element.55.rows_ref, f32[2304]{0:T(1024)} %get-tuple-element.51.gates_ref, bf16[1,4,32,96,4096]{4,3,2,1,0:T(8,128)(2,1)} %rest_1_.15, bf16[1,4,32,96,4096]{4,3,2,1,0:T(8,128)(2,1)} %rest_1_.15, ...), custom_call_target="tpu_custom_call" | custom-call | flops 8000000000 | bytes 18874368 | tf_op jit(solution)/shard_map/combine/pallas_call | solution.py:260
  34.7 9.3 %pick.7 = (bf16[32,24,4096]{2,1,0:T(8,128)(2,1)}, bf16[32,24,4096]{2,1,0:T(8,128)(2,1)}) custom-call(s32[2]{0:T(128)} %pad_add_fusion.1.owners_ref, bf16[1,4,32,96,4096]{4,3,2,1,0:T(8,128)(2,1)} %rest_1_.15, bf16[1,4,32,96,4096]{4,3,2,1,0:T(8,128)(2,1)} %rest_1_.15, f32[12288,128]{1,0:T(8,128)} %combine.8.refs_2_), custom_call_target="tpu_custom_call" | custom-call | flops 4000000000 | bytes 25165824 | tf_op jit(solution)/shard_map/pick/pallas_call | solution.py:195
  44.0 13.5 %combine.9 = (f32[4096,128]{1,0:T(8,128)}, f32[4096,128]{1,0:T(8,128)}, f32[4096,128]{1,0:T(8,128)}) custom-call(s32[1]{0:T(128)} %bitcast.6.owner_ref, s32[2304]{0:T(1024)} %get-tuple-element.54.rows_ref, f32[2304]{0:T(1024)} %get-tuple-element.50.gates_ref, bf16[1,4,32,96,4096]{4,3,2,1,0:T(8,128)(2,1)} %rest_1_.15, bf16[1,4,32,96,4096]{4,3,2,1,0:T(8,128)(2,1)} %rest_1_.15, ...), custom_call_target="tpu_custom_call" | custom-call | flops 8000000000 | bytes 18874368 | tf_op jit(solution)/shard_map/combine/pallas_call | solution.py:260
  57.5 9.5 %pick.8 = (bf16[32,24,4096]{2,1,0:T(8,128)(2,1)}, bf16[32,24,4096]{2,1,0:T(8,128)(2,1)}) custom-call(s32[2]{0:T(128)} %pad_add_fusion.1.owners_ref, bf16[1,4,32,96,4096]{4,3,2,1,0:T(8,128)(2,1)} %rest_1_.15, bf16[1,4,32,96,4096]{4,3,2,1,0:T(8,128)(2,1)} %rest_1_.15, f32[4096,128]{1,0:T(8,128)} %get-tuple-element.29.refs_2_), custom_call_target="tpu_custom_call" | custom-call | flops 4000000000 | bytes 25165824 | tf_op jit(solution)/shard_map/pick/pallas_call | solution.py:195
  77.2 12.6 %combine.10 = (f32[6144,128]{1,0:T(8,128)}, f32[6144,128]{1,0:T(8,128)}) custom-call(s32[1]{0:T(128)} %bitcast.6.owner_ref, s32[2304]{0:T(1024)} %get-tuple-element.56.rows_ref, f32[2304]{0:T(1024)} %get-tuple-element.52.gates_ref, bf16[1,4,32,96,4096]{4,3,2,1,0:T(8,128)(2,1)} %rest_1_.15, bf16[1,4,32,96,4096]{4,3,2,1,0:T(8,128)(2,1)} %rest_1_.15, ...), custom_call_target="tpu_custom_call" | custom-call | flops 8000000000 | bytes 18874368 | tf_op jit(solution)/shard_map/combine/pallas_call | solution.py:260
  89.8 9.3 %pick.9 = (bf16[32,24,4096]{2,1,0:T(8,128)(2,1)}, bf16[32,24,4096]{2,1,0:T(8,128)(2,1)}) custom-call(s32[2]{0:T(128)} %pad_add_fusion.owners_ref, bf16[1,4,32,96,4096]{4,3,2,1,0:T(8,128)(2,1)} %rest_1_.15, bf16[1,4,32,96,4096]{4,3,2,1,0:T(8,128)(2,1)} %rest_1_.15, f32[6144,128]{1,0:T(8,128)} %get-tuple-element.31.refs_2_), custom_call_target="tpu_custom_call" | custom-call | flops 4000000000 | bytes 25165824 | tf_op jit(solution)/shard_map/pick/pallas_call | solution.py:195
  101.0 13.5 %combine.11 = (f32[4096,128]{1,0:T(8,128)}, f32[4096,128]{1,0:T(8,128)}, f32[4096,128]{1,0:T(8,128)}) custom-call(s32[1]{0:T(128)} %bitcast.6.owner_ref, s32[2304]{0:T(1024)} %get-tuple-element.53.rows_ref, f32[2304]{0:T(1024)} %get-tuple-element.49.gates_ref, bf16[1,4,32,96,4096]{4,3,2,1,0:T(8,128)(2,1)} %rest_1_.15, ...), custom_call_target="tpu_custom_call" | custom-call | flops 8000000000 | bytes 18874368 | tf_op jit(solution)/shard_map/combine/pallas_call | solution.py:260
  114.6 46.5 %gated.2.hidden_ref = bf16[768,2816]{1,0:T(8,128)(2,1)} custom-call(bf16[1536,4096]{1,0:T(8,128)(2,1)} %bitcast.122, f32[1,4096]{1,0:T(1,128)} %gain_ref.3, bf16[4096,2816]{1,0:T(8,128)(2,1)} %bitcast.148, bf16[4096,2816]{1,0:T(8,128)(2,1)} %bitcast.150, f32[4096,128]{1,0:T(8,128)} %get-tuple-element.34.rest_0_), custom_call_target="tpu_custom_call" | custom-call | flops 35433480192 | bytes 46137344 | tf_op jit(solution)/shard_map/gated/pallas_call | solution.py:77
  161.1 23.3 %down.2.rest_4_.sh_ref = bf16[768,4096]{1,0:T(8,128)(2,1)} custom-call(bf16[768,2816]{1,0:T(8,128)(2,1)} %gated.2.hidden_ref, bf16[2816,4096]{1,0:T(8,128)(2,1)} %bitcast.152), custom_call_target="tpu_custom_call" | custom-call | flops 17716740096 | bytes 23068672 | tf_op jit(solution)/shard_map/down/pallas_call | solution.py:111
  184.3 12.2 %combine.12.own_ref.rest_0_ = f32[12288,128]{1,0:T(8,128)} custom-call(s32[1]{0:T(128)} %bitcast.owner_ref, s32[2304]{0:T(1024)} %squeeze.91.rows_ref, f32[2304]{0:T(1024)} %squeeze.92.gates_ref, bf16[1,4,32,96,4096]{4,3,2,1,0:T(8,128)(2,1)} %rest_1_.15, bf16[1,4,32,96,4096]{4,3,2,1,0:T(8,128)(2,1)} %rest_1_.15, ...), custom_call_target="tpu_custom_call" | custom-call | flops 8000000000 | bytes 18874368 | tf_op jit(solution)/shard_map/combine/pallas_call | solution.py:260
  196.5 16.9 %collective-permute-done.8.far_ref = f32[12288,128]{1,0:T(8,128)} collective-permute-done((f32[12288,128]{1,0:T(8,128)}, f32[12288,128]{1,0:T(8,128)}, u32[]{:S(2)}, u32[]{:S(2)}) %collective-permute-start.8) | collective-permute-done | bytes 6291488 | tf_op jit(solution)/shard_map/ppermute | solution.py:364
  221.9 46.0 %gated.3.rest_4_.hidden_ref = bf16[768,2816]{1,0:T(8,128)(2,1)} custom-call(bf16[1536,4096]{1,0:T(8,128)(2,1)} %bitcast.124, f32[1,4096]{1,0:T(1,128)} %gain_ref.3, bf16[4096,2816]{1,0:T(8,128)(2,1)} %bitcast.149, bf16[4096,2816]{1,0:T(8,128)(2,1)} %bitcast.151, bf16[384,4096]{1,0:T(8,128)(2,1)} %finish.9.rest_0_), custom_call_target="tpu_custom_call" | custom-call | flops 35433480192 | bytes 46137344 | tf_op jit(solution)/shard_map/gated/pallas_call | solution.py:77
  269.8 13.5 %combine.13 = (f32[4096,128]{1,0:T(8,128)}, f32[4096,128]{1,0:T(8,128)}, f32[4096,128]{1,0:T(8,128)}) custom-call(s32[1]{0:T(128)} %bitcast.owner_ref, s32[2304]{0:T(1024)} %squeeze.87.rows_ref, f32[2304]{0:T(1024)} %squeeze.88.gates_ref, bf16[1,4,32,96,4096]{4,3,2,1,0:T(8,128)(2,1)} %rest_1_.15, bf16[1,4,32,96,4096]{4,3,2,1,0:T(8,128)(2,1)} %rest_1_.15, ...), custom_call_target="tpu_custom_call" | custom-call | flops 8000000000 | bytes 18874368 | tf_op jit(solution)/shard_map/combine/pallas_call | solution.py:260
  288.7 14.6 %collective-permute-done.11.far_ref = f32[4096,128]{1,0:T(8,128)} collective-permute-done((f32[4096,128]{1,0:T(8,128)}, f32[4096,128]{1,0:T(8,128)}, u32[]{:S(2)}, u32[]{:S(2)}) %collective-permute-start.11) | collective-permute-done | bytes 2097184 | tf_op jit(solution)/shard_map/ppermute | solution.py:364
  309.0 23.4 %down.3.rest_4_.sh_ref = bf16[768,4096]{1,0:T(8,128)(2,1)} custom-call(bf16[768,2816]{1,0:T(8,128)(2,1)} %gated.3.rest_4_.hidden_ref, bf16[2816,4096]{1,0:T(8,128)(2,1)} %bitcast.153, bf16[128,4096]{1,0:T(8,128)(2,1)} %finish.11.rest_0_), custom_call_target="tpu_custom_call" | custom-call | flops 17716740096 | bytes 23068672 | tf_op jit(solution)/shard_map/down/pallas_call | solution.py:111
  332.6 12.6 %combine.14 = (f32[6144,128]{1,0:T(8,128)}, f32[6144,128]{1,0:T(8,128)}) custom-call(s32[1]{0:T(128)} %bitcast.owner_ref, s32[2304]{0:T(1024)} %squeeze.96.rows_ref, f32[2304]{0:T(1024)} %squeeze.97.gates_ref, bf16[1,4,32,96,4096]{4,3,2,1,0:T(8,128)(2,1)} %rest_1_.15, bf16[1,4,32,96,4096]{4,3,2,1,0:T(8,128)(2,1)} %rest_1_.15, ...), custom_call_target="tpu_custom_call" | custom-call | flops 8000000000 | bytes 18874368 | tf_op jit(solution)/shard_map/combine/pallas_call | solution.py:260
  356.3 13.6 %combine.15 = (f32[4096,128]{1,0:T(8,128)}, f32[4096,128]{1,0:T(8,128)}, f32[4096,128]{1,0:T(8,128)}) custom-call(s32[1]{0:T(128)} %bitcast.owner_ref, s32[2304]{0:T(1024)} %squeeze.76.rows_ref, f32[2304]{0:T(1024)} %squeeze.78.gates_ref, bf16[1,4,32,96,4096]{4,3,2,1,0:T(8,128)(2,1)} %rest_1_.15, bf16[1,4,32,96,4096]{4,3,2,1,0:T(8,128)(2,1)} %rest_1_.15, ...), custom_call_target="tpu_custom_call" | custom-call | flops 8000000000 | bytes 18874368 | tf_op jit(solution)/shard_map/combine/pallas_call | solution.py:260
  377.1 22.3 %collective-permute-done.15.refs_1_.rest_0_ = bf16[128,4096]{1,0:T(8,128)(2,1)S(1)} collective-permute-done((bf16[128,4096]{1,0:T(8,128)(2,1)}, bf16[128,4096]{1,0:T(8,128)(2,1)S(1)}, u32[]{:S(2)}, u32[]{:S(2)}) %collective-permute-start.15) | collective-permute-done | bytes 1048608 | tf_op jit(solution)/shard_map/ppermute | solution.py:387
  401.4 19.7 %collective-permute-done.17.refs_3_.rest_2_ = bf16[128,4096]{1,0:T(8,128)(2,1)S(1)} collective-permute-done((bf16[128,4096]{1,0:T(8,128)(2,1)}, bf16[128,4096]{1,0:T(8,128)(2,1)S(1)}, u32[]{:S(2)}, u32[]{:S(2)}) %collective-permute-start.17) | collective-permute-done | bytes 1048608 | tf_op jit(solution)/shard_map/ppermute | solution.py:387
  430.6 33.2 %fusion.33.rest_0_.rest_2_.v_ref = bf16[768,4096]{1,0:T(8,128)(2,1)} fusion(bf16[768,4096]{1,0:T(8,128)(2,1)} %normalize.3, bf16[512,8,32,128]{3,2,1,0:T(8,128)(2,1)} %bitcast.139), kind=kOutput, calls=%fused_computation.29 | convolution fusion | flops 25772949504 | bytes 46137344 | tf_op jit(solution)/shard_map/dot_general | solution.py:392
  470.6 35.7 %fusion.30.rest_1_.k_ref = bf16[768,4096]{1,0:T(8,128)(2,1)} fusion(bf16[768,4096]{1,0:T(8,128)(2,1)} %normalize.3, bf16[512,8,32,128]{3,2,1,0:T(8,128)(2,1)} %bitcast.142), kind=kOutput, calls=%fused_computation.28 | convolution fusion | flops 25772949504 | bytes 46137344 | tf_op jit(solution)/shard_map/dot_general | solution.py:392
  506.3 31.4 %fusion.27.rest_0_.q_ref = bf16[768,4096]{1,0:T(8,128)(2,1)} fusion(bf16[768,4096]{1,0:T(8,128)(2,1)S(1)} %bitcast.138, bf16[512,8,32,128]{3,2,1,0:T(8,128)(2,1)} %bitcast.145), kind=kOutput, calls=%fused_computation.27 | convolution fusion | flops 25772949504 | bytes 46137344 | tf_op jit(solution)/shard_map/dot_general | solution.py:392
  543.8 25.4 %attend.4.rest_3_ = bf16[4,384,4096]{2,1,0:T(8,128)(2,1)} custom-call(bf16[768,4096]{1,0:T(8,128)(2,1)} %fusion.27.rest_0_.q_ref, bf16[768,4096]{1,0:T(8,128)(2,1)} %fusion.30.rest_1_.k_ref, bf16[768,4096]{1,0:T(8,128)(2,1)} %fusion.33.rest_0_.rest_2_.v_ref, bf16[4096,4096]{1,0:T(8,128)(2,1)} %bitcast.133, ...), custom_call_target="tpu_custom_call" | custom-call | flops 12884901888 | bytes 33554432 | tf_op jit(solution)/shard_map/attend/pallas_call | solution.py:168
  569.2 25.1 %attend.5.rest_0_.rest_3_ = bf16[4,384,4096]{2,1,0:T(8,128)(2,1)} custom-call(bf16[768,4096]{1,0:T(8,128)(2,1)} %fusion.27.rest_0_.q_ref, bf16[768,4096]{1,0:T(8,128)(2,1)} %fusion.30.rest_1_.k_ref, bf16[768,4096]{1,0:T(8,128)(2,1)} %fusion.33.rest_0_.rest_2_.v_ref, bf16[4096,4096]{1,0:T(8,128)(2,1)} %bitcast.134, ...), custom_call_target="tpu_custom_call", output_to_operand_aliasing={{}: (7, {})} | custom-call | flops 12884901888 | bytes 33554432 | tf_op jit(solution)/shard_map/attend/pallas_call | solution.py:168
  606.0 21.7 %fusion.42.rest_0_.k_ref = bf16[384,4096]{1,0:T(8,128)(2,1)} fusion(bf16[384,4096]{1,0:T(8,128)(2,1)} %normalize.4, bf16[512,8,32,128]{3,2,1,0:T(8,128)(2,1)} %bitcast.143), kind=kOutput, calls=%fused_computation.32 | convolution fusion | flops 12886474752 | bytes 39845888 | tf_op jit(solution)/shard_map/dot_general | solution.py:392
  627.8 21.5 %fusion.48.rest_0_.v_ref = bf16[384,4096]{1,0:T(8,128)(2,1)} fusion(bf16[384,4096]{1,0:T(8,128)(2,1)} %normalize.4, bf16[512,8,32,128]{3,2,1,0:T(8,128)(2,1)} %bitcast.140), kind=kOutput, calls=%fused_computation.34 | convolution fusion | flops 12886474752 | bytes 39845888 | tf_op jit(solution)/shard_map/dot_general | solution.py:392
  653.4 21.5 %fusion.36.q_ref = bf16[384,4096]{1,0:T(8,128)(2,1)} fusion(bf16[384,4096]{1,0:T(8,128)(2,1)} %normalize.4, bf16[512,8,32,128]{3,2,1,0:T(8,128)(2,1)} %bitcast.146), kind=kOutput, calls=%fused_computation.30 | convolution fusion | flops 12886474752 | bytes 39845888 | tf_op jit(solution)/shard_map/dot_general | solution.py:392
  680.5 25.1 %attend.6.refs_4_.rest_3_ = bf16[4,384,4096]{2,1,0:T(8,128)(2,1)} custom-call(bf16[384,4096]{1,0:T(8,128)(2,1)} %fusion.36.q_ref, bf16[384,4096]{1,0:T(8,128)(2,1)} %fusion.42.rest_0_.k_ref, bf16[384,4096]{1,0:T(8,128)(2,1)} %fusion.48.rest_0_.v_ref, bf16[4096,4096]{1,0:T(8,128)(2,1)} %bitcast.135, ...), custom_call_target="tpu_custom_call", output_to_operand_aliasing={{}: (7, {})} | custom-call | flops 12884901888 | bytes 33554432 | tf_op jit(solution)/shard_map/attend/pallas_call | solution.py:168
  712.9 21.5 %fusion.51.v_ref = bf16[384,4096]{1,0:T(8,128)(2,1)} fusion(bf16[384,4096]{1,0:T(8,128)(2,1)} %normalize.5, bf16[512,8,32,128]{3,2,1,0:T(8,128)(2,1)} %bitcast.141), kind=kOutput, calls=%fused_computation.35 | convolution fusion | flops 12886474752 | bytes 39845888 | tf_op jit(solution)/shard_map/dot_general | solution.py:392
  734.4 20.9 %fusion.45.k_ref = bf16[384,4096]{1,0:T(8,128)(2,1)} fusion(bf16[384,4096]{1,0:T(8,128)(2,1)S(1)} %copy-done.6, bf16[512,8,32,128]{3,2,1,0:T(8,128)(2,1)} %bitcast.144), kind=kOutput, calls=%fused_computation.33 | convolution fusion | flops 12886474752 | bytes 39845888 | tf_op jit(solution)/shard_map/dot_general | solution.py:392
  755.3 20.5 %fusion.39.q_ref = bf16[384,4096]{1,0:T(8,128)(2,1)} fusion(bf16[384,4096]{1,0:T(8,128)(2,1)S(1)} %copy-done.6, bf16[512,8,32,128]{3,2,1,0:T(8,128)(2,1)} %bitcast.147), kind=kOutput, calls=%fused_computation.31 | convolution fusion | flops 12886474752 | bytes 39845888 | tf_op jit(solution)/shard_map/dot_general | solution.py:392
  775.8 25.1 %attend.7 = bf16[4,384,4096]{2,1,0:T(8,128)(2,1)} custom-call(bf16[384,4096]{1,0:T(8,128)(2,1)} %fusion.39.q_ref, bf16[384,4096]{1,0:T(8,128)(2,1)} %fusion.45.k_ref, bf16[384,4096]{1,0:T(8,128)(2,1)} %fusion.51.v_ref, bf16[4096,4096]{1,0:T(8,128)(2,1)} %bitcast.136, bf16[128,4096]{1,0:T(8,128)(2,1)} %copy-done.4, ...), custom_call_target="tpu_custom_call", output_to_operand_aliasing={{}: (7, {})} | custom-call | flops 12884901888 | bytes 33554432 | tf_op jit(solution)/shard_map/attend/pallas_call | solution.py:168
  (133 shorter events, 127.8 us)
Async XLA Ops:
  4.8 17.8 %collective-permute-start.1 = (bf16[32,24,4096]{2,1,0:T(8,128)(2,1)}, bf16[32,24,4096]{2,1,0:T(8,128)(2,1)}, u32[]{:S(2)}, u32[]{:S(2)}) collective-permute-start(bf16[32,24,4096]{2,1,0:T(8,128)(2,1)} %pick.5.refs_1_), channel_id=1, source_target_pairs={{0,1},{1,0},{2,3},{3,2},{4,5},{5,4},{6,7},{7,6}} | collective-permute-start | bytes 18874376 | tf_op jit(solution)/shard_map/ppermute | solution.py:354
  10.4 33.6 %collective-permute-start.3 = (bf16[32,24,4096]{2,1,0:T(8,128)(2,1)}, bf16[32,24,4096]{2,1,0:T(8,128)(2,1)}, u32[]{:S(2)}, u32[]{:S(2)}) collective-permute-start(bf16[32,24,4096]{2,1,0:T(8,128)(2,1)} %pick.6.rest_4_), channel_id=1, source_target_pairs={{0,1},{1,0},{2,3},{3,2},{4,5},{5,4},{6,7},{7,6}} | collective-permute-start | bytes 18874376 | tf_op jit(solution)/shard_map/ppermute | solution.py:354
  15.7 5.4 collective-permute-start
  44.0 32.7 %collective-permute-start.2 = (bf16[32,24,4096]{2,1,0:T(8,128)(2,1)}, bf16[32,24,4096]{2,1,0:T(8,128)(2,1)}, u32[]{:S(2)}, u32[]{:S(2)}) collective-permute-start(bf16[32,24,4096]{2,1,0:T(8,128)(2,1)} %get-tuple-element.27), channel_id=1, source_target_pairs={{0,1},{1,0},{2,3},{3,2},{4,5},{5,4},{6,7},{7,6}} | collective-permute-start | bytes 18874376 | tf_op jit(solution)/shard_map/ppermute | solution.py:354
  67.0 32.1 %collective-permute-start.7 = (bf16[32,24,4096]{2,1,0:T(8,128)(2,1)}, bf16[32,24,4096]{2,1,0:T(8,128)(2,1)}, u32[]{:S(2)}, u32[]{:S(2)}) collective-permute-start(bf16[32,24,4096]{2,1,0:T(8,128)(2,1)} %get-tuple-element.33), channel_id=1, source_target_pairs={{0,1},{1,0},{2,3},{3,2},{4,5},{5,4},{6,7},{7,6}} | collective-permute-start | bytes 18874376 | tf_op jit(solution)/shard_map/ppermute | solution.py:354
  74.7 138.7 %collective-permute-start.8 = (f32[12288,128]{1,0:T(8,128)}, f32[12288,128]{1,0:T(8,128)}, u32[]{:S(2)}, u32[]{:S(2)}) collective-permute-start(f32[12288,128]{1,0:T(8,128)} %combine.8.refs_2_), channel_id=1, source_target_pairs={{0,2},{1,3},{2,0},{3,1},{4,6},{5,7},{6,4},{7,5}} | collective-permute-start | bytes 18874376 | tf_op jit(solution)/shard_map/ppermute | solution.py:364
  76.6 206.7 %collective-permute-start.12 = (f32[4096,128]{1,0:T(8,128)}, f32[4096,128]{1,0:T(8,128)}, u32[]{:S(2)}, u32[]{:S(2)}) collective-permute-start(f32[4096,128]{1,0:T(8,128)} %get-tuple-element.29.refs_2_), channel_id=1, source_target_pairs={{0,2},{1,3},{2,0},{3,1},{4,6},{5,7},{6,4},{7,5}} | collective-permute-start | bytes 6291464 | tf_op jit(solution)/shard_map/ppermute | solution.py:364
  76.7 107.6 %collective-permute-start.6 = (bf16[32,24,4096]{2,1,0:T(8,128)(2,1)}, bf16[32,24,4096]{2,1,0:T(8,128)(2,1)}, u32[]{:S(2)}, u32[]{:S(2)}) collective-permute-start(bf16[32,24,4096]{2,1,0:T(8,128)(2,1)} %get-tuple-element.28.rest_4_), channel_id=1, source_target_pairs={{0,1},{1,0},{2,3},{3,2},{4,5},{5,4},{6,7},{7,6}} | collective-permute-start | bytes 18874376 | tf_op jit(solution)/shard_map/ppermute | solution.py:354
  76.7 191.2 %collective-permute-start.5 = (bf16[32,24,4096]{2,1,0:T(8,128)(2,1)}, bf16[32,24,4096]{2,1,0:T(8,128)(2,1)}, u32[]{:S(2)}, u32[]{:S(2)}) collective-permute-start(bf16[32,24,4096]{2,1,0:T(8,128)(2,1)} %get-tuple-element.30.rest_4_), channel_id=1, source_target_pairs={{0,1},{1,0},{2,3},{3,2},{4,5},{5,4},{6,7},{7,6}} | collective-permute-start | bytes 18874376 | tf_op jit(solution)/shard_map/ppermute | solution.py:354
  99.2 204.1 %collective-permute-start.11 = (f32[4096,128]{1,0:T(8,128)}, f32[4096,128]{1,0:T(8,128)}, u32[]{:S(2)}, u32[]{:S(2)}) collective-permute-start(f32[4096,128]{1,0:T(8,128)} %get-tuple-element.39), channel_id=1, source_target_pairs={{0,2},{1,3},{2,0},{3,1},{4,6},{5,7},{6,4},{7,5}} | collective-permute-start | bytes 6291464 | tf_op jit(solution)/shard_map/ppermute | solution.py:364
  184.3 148.1 %collective-permute-start.10 = (bf16[32,24,4096]{2,1,0:T(8,128)(2,1)}, bf16[32,24,4096]{2,1,0:T(8,128)(2,1)}, u32[]{:S(2)}, u32[]{:S(2)}) collective-permute-start(bf16[32,24,4096]{2,1,0:T(8,128)(2,1)} %get-tuple-element.37), channel_id=1, source_target_pairs={{0,1},{1,0},{2,3},{3,2},{4,5},{5,4},{6,7},{7,6}} | collective-permute-start | bytes 18874376 | tf_op jit(solution)/shard_map/ppermute | solution.py:354
  213.4 141.4 %collective-permute-start.4 = (bf16[32,24,4096]{2,1,0:T(8,128)(2,1)}, bf16[32,24,4096]{2,1,0:T(8,128)(2,1)}, u32[]{:S(2)}, u32[]{:S(2)}) collective-permute-start(bf16[32,24,4096]{2,1,0:T(8,128)(2,1)} %get-tuple-element.32.rest_4_), channel_id=1, source_target_pairs={{0,1},{1,0},{2,3},{3,2},{4,5},{5,4},{6,7},{7,6}} | collective-permute-start | bytes 18874376 | tf_op jit(solution)/shard_map/ppermute | solution.py:354
  267.9 79.5 %collective-permute-start.9 = (f32[4096,128]{1,0:T(8,128)}, f32[4096,128]{1,0:T(8,128)}, u32[]{:S(2)}, u32[]{:S(2)}) collective-permute-start(f32[4096,128]{1,0:T(8,128)} %get-tuple-element.36), channel_id=1, source_target_pairs={{0,2},{1,3},{2,0},{3,1},{4,6},{5,7},{6,4},{7,5}} | collective-permute-start | bytes 6291464 | tf_op jit(solution)/shard_map/ppermute | solution.py:364
  283.3 116.3 %collective-permute-start.14 = (bf16[384,4096]{1,0:T(8,128)(2,1)}, bf16[384,4096]{1,0:T(8,128)(2,1)}, u32[]{:S(2)}, u32[]{:S(2)}) collective-permute-start(bf16[384,4096]{1,0:T(8,128)(2,1)} %finish.9.rest_0_), channel_id=1, source_target_pairs={{0,4},{4,0},{1,5},{5,1},{2,6},{6,2},{3,7},{7,3}} | collective-permute-start | bytes 9437192 | tf_op jit(solution)/shard_map/ppermute | solution.py:387
  307.2 69.8 %collective-permute-start.16 = (bf16[128,4096]{1,0:T(8,128)(2,1)}, bf16[128,4096]{1,0:T(8,128)(2,1)S(1)}, u32[]{:S(2)}, u32[]{:S(2)}) collective-permute-start(bf16[128,4096]{1,0:T(8,128)(2,1)} %finish.11.rest_0_), channel_id=1, source_target_pairs={{0,4},{4,0},{1,5},{5,1},{2,6},{6,2},{3,7},{7,3}} | collective-permute-start | bytes 3145736 | tf_op jit(solution)/shard_map/ppermute | solution.py:387
  332.4 67.0 %collective-permute-start.15 = (bf16[128,4096]{1,0:T(8,128)(2,1)}, bf16[128,4096]{1,0:T(8,128)(2,1)S(1)}, u32[]{:S(2)}, u32[]{:S(2)}) collective-permute-start(bf16[128,4096]{1,0:T(8,128)(2,1)} %finish.10.rest_0_), channel_id=1, source_target_pairs={{0,4},{4,0},{1,5},{5,1},{2,6},{6,2},{3,7},{7,3}} | collective-permute-start | bytes 3145736 | tf_op jit(solution)/shard_map/ppermute | solution.py:387
  351.3 69.8 %collective-permute-start.17 = (bf16[128,4096]{1,0:T(8,128)(2,1)}, bf16[128,4096]{1,0:T(8,128)(2,1)S(1)}, u32[]{:S(2)}, u32[]{:S(2)}) collective-permute-start(bf16[128,4096]{1,0:T(8,128)(2,1)} %finish.12.rest_4_), channel_id=1, source_target_pairs={{0,4},{4,0},{1,5},{5,1},{2,6},{6,2},{3,7},{7,3}} | collective-permute-start | bytes 3145736 | tf_op jit(solution)/shard_map/ppermute | solution.py:387
  354.9 109.0 %collective-permute-start.19 = (f32[6144,128]{1,0:T(8,128)}, f32[6144,128]{1,0:T(8,128)}, u32[]{:S(2)}, u32[]{:S(2)}) collective-permute-start(f32[6144,128]{1,0:T(8,128)} %get-tuple-element.31.refs_2_), channel_id=1, source_target_pairs={{0,2},{1,3},{2,0},{3,1},{4,6},{5,7},{6,4},{7,5}} | collective-permute-start | bytes 9437192 | tf_op jit(solution)/shard_map/ppermute | solution.py:364
  376.9 44.5 %copy-start.1 = (bf16[128,4096]{1,0:T(8,128)(2,1)}, bf16[128,4096]{1,0:T(8,128)(2,1)S(1)}, u32[]{:S(2)}) copy-start(bf16[128,4096]{1,0:T(8,128)(2,1)S(1)} %collective-permute-done.16.refs_2_.rest_1_) | copy-start | bytes 3145732
  376.9 217.3 %collective-permute-start.13 = (f32[4096,128]{1,0:T(8,128)}, f32[4096,128]{1,0:T(8,128)}, u32[]{:S(2)}, u32[]{:S(2)}) collective-permute-start(f32[4096,128]{1,0:T(8,128)} %get-tuple-element.34.rest_0_), channel_id=1, source_target_pairs={{0,2},{1,3},{2,0},{3,1},{4,6},{5,7},{6,4},{7,5}} | collective-permute-start | bytes 6291464 | tf_op jit(solution)/shard_map/ppermute | solution.py:364
  399.4 22.0 %copy-start.2 = (bf16[128,4096]{1,0:T(8,128)(2,1)}, bf16[128,4096]{1,0:T(8,128)(2,1)S(1)}, u32[]{:S(2)}) copy-start(bf16[128,4096]{1,0:T(8,128)(2,1)S(1)} %collective-permute-done.15.refs_1_.rest_0_) | copy-start | bytes 3145732
  399.4 139.1 %collective-permute-start.18 = (f32[6144,128]{1,0:T(8,128)}, f32[6144,128]{1,0:T(8,128)}, u32[]{:S(2)}, u32[]{:S(2)}) collective-permute-start(f32[6144,128]{1,0:T(8,128)} %get-tuple-element.44), channel_id=1, source_target_pairs={{0,2},{1,3},{2,0},{3,1},{4,6},{5,7},{6,4},{7,5}} | collective-permute-start | bytes 9437192 | tf_op jit(solution)/shard_map/ppermute | solution.py:364
  399.6 249.7 %collective-permute-start.21 = (f32[4096,128]{1,0:T(8,128)}, f32[4096,128]{1,0:T(8,128)}, u32[]{:S(2)}, u32[]{:S(2)}) collective-permute-start(f32[4096,128]{1,0:T(8,128)} %get-tuple-element.46), channel_id=1, source_target_pairs={{0,2},{1,3},{2,0},{3,1},{4,6},{5,7},{6,4},{7,5}} | collective-permute-start | bytes 6291464 | tf_op jit(solution)/shard_map/ppermute | solution.py:364
  421.1 253.7 %collective-permute-start.25 = (f32[4096,128]{1,0:T(8,128)}, f32[4096,128]{1,0:T(8,128)}, u32[]{:S(2)}, u32[]{:S(2)}) collective-permute-start(f32[4096,128]{1,0:T(8,128)} %get-tuple-element.48), channel_id=1, source_target_pairs={{0,2},{1,3},{2,0},{3,1},{4,6},{5,7},{6,4},{7,5}} | collective-permute-start | bytes 6291464 | tf_op jit(solution)/shard_map/ppermute | solution.py:364
  463.9 42.4 %slice-start = ((s8[6291456]{0:T(1024)(128)(4,1)}), s8[2097152]{0:T(1024)(128)(4,1)S(1)}, s32[]{:S(2)}) async-start(s8[6291456]{0:T(1024)(128)(4,1)} %bitcast.137), calls=%async_computation | async-start | bytes 4194304
  469.0 130.9 %collective-permute-start.22 = (bf16[192,4096]{1,0:T(8,128)(2,1)}, bf16[192,4096]{1,0:T(8,128)(2,1)}, u32[]{:S(2)}, u32[]{:S(2)}) collective-permute-start(bf16[192,4096]{1,0:T(8,128)(2,1)} %finish.13.rest_3_), channel_id=1, source_target_pairs={{0,4},{4,0},{1,5},{5,1},{2,6},{6,2},{3,7},{7,3}} | collective-permute-start | bytes 4718600 | tf_op jit(solution)/shard_map/ppermute | solution.py:387
  470.6 35.7 %slice-start.1 = ((s8[6291456]{0:T(1024)(128)(4,1)}), s8[4194304]{0:T(1024)(128)(4,1)S(1)}, s32[]{:S(2)}) async-start(s8[6291456]{0:T(1024)(128)(4,1)} %bitcast.137), calls=%async_computation.1 | async-start | bytes 8388608
  543.5 56.5 %collective-permute-start.23 = (bf16[192,4096]{1,0:T(8,128)(2,1)}, bf16[192,4096]{1,0:T(8,128)(2,1)S(1)}, u32[]{:S(2)}, u32[]{:S(2)}) collective-permute-start(bf16[192,4096]{1,0:T(8,128)(2,1)} %finish.14.rest_1_), channel_id=1, source_target_pairs={{0,4},{4,0},{1,5},{5,1},{2,6},{6,2},{3,7},{7,3}} | collective-permute-start | bytes 4718600 | tf_op jit(solution)/shard_map/ppermute | solution.py:387
  598.2 107.4 %collective-permute-start.20 = (bf16[128,4096]{1,0:T(8,128)(2,1)}, bf16[128,4096]{1,0:T(8,128)(2,1)S(1)}, u32[]{:S(2)}, u32[]{:S(2)}) collective-permute-start(bf16[128,4096]{1,0:T(8,128)(2,1)} %finish.15.refs_3_), channel_id=1, source_target_pairs={{0,4},{4,0},{1,5},{5,1},{2,6},{6,2},{3,7},{7,3}} | collective-permute-start | bytes 3145736 | tf_op jit(solution)/shard_map/ppermute | solution.py:387
  653.1 52.5 %collective-permute-start.24 = (bf16[128,4096]{1,0:T(8,128)(2,1)}, bf16[128,4096]{1,0:T(8,128)(2,1)S(1)}, u32[]{:S(2)}, u32[]{:S(2)}) collective-permute-start(bf16[128,4096]{1,0:T(8,128)(2,1)} %finish.16.rest_1_), channel_id=1, source_target_pairs={{0,4},{4,0},{1,5},{5,1},{2,6},{6,2},{3,7},{7,3}} | collective-permute-start | bytes 3145736 | tf_op jit(solution)/shard_map/ppermute | solution.py:387
  678.7 26.9 %collective-permute-start.26 = (bf16[128,4096]{1,0:T(8,128)(2,1)}, bf16[128,4096]{1,0:T(8,128)(2,1)}, u32[]{:S(2)}, u32[]{:S(2)}) collective-permute-start(bf16[128,4096]{1,0:T(8,128)(2,1)} %finish.17.rest_2_), channel_id=1, source_target_pairs={{0,4},{4,0},{1,5},{5,1},{2,6},{6,2},{3,7},{7,3}} | collective-permute-start | bytes 3145736 | tf_op jit(solution)/shard_map/ppermute | solution.py:387
  712.9 21.5 %copy-start.6 = (bf16[384,4096]{1,0:T(8,128)(2,1)S(1)}, bf16[384,4096]{1,0:T(8,128)(2,1)}, u32[]{:S(2)}) copy-start(bf16[384,4096]{1,0:T(8,128)(2,1)} %normalize.5) | copy-start | bytes 9437188
  (11 other events, 56.2 us)

commit v3 on v2

--- a/solution.py
+++ b/solution.py
@@ -123,17 +123,18 @@
     )(hidden, w_down, *deps)
 
 
-def attend(queries, keys, values, row_block, blocks, w_out, micro, micro_count, seq_len, head_dim, previous=None, deps=()):
+def attend(queries, keys, values, blocks, w_out, micro, each, micro_count, seq_len, head_dim, previous=None, deps=()):
     width = queries.shape[1]
     dim = w_out.shape[1]
     cols = 1024
-    group = 8
+    group = 8 * each // queries.shape[0]
     pair = 2 * seq_len
     core_steps = width // (group * head_dim)
     scale = 1.0 / math.sqrt(head_dim)
     sizes = [block.shape[0] for block in blocks]
     starts = [sum(sizes[:c]) for c in range(len(sizes))]
     tokens = sum(sizes)
+    micros = tokens // each
 
     def body(q_ref, k_ref, v_ref, w_ref, *rest):
         y_refs = rest[:len(blocks)]
@@ -159,19 +160,19 @@
             proj = jnp.dot(mixed[...], w_ref[...], preferred_element_type=jnp.float32).astype(jnp.bfloat16)
             for ref, start, size in zip(y_refs, starts, sizes):
                 part = proj[start:start + size].astype(jnp.float32)
-                out_ref[0, start:start + size, :] = (ref[...].astype(jnp.float32) + part).astype(jnp.bfloat16)
-
-    core_spec = pl.BlockSpec((tokens, group * head_dim), lambda s: (row_block, jnp.minimum(s, core_steps - 1)))
+                out_ref[start // each, start % each:start % each + size, :] = (ref[...].astype(jnp.float32) + part).astype(jnp.bfloat16)
+
+    core_spec = pl.BlockSpec((tokens, group * head_dim), lambda s: (0, jnp.minimum(s, core_steps - 1)))
     tail = lambda s: jnp.maximum(s - core_steps, 0)
     extra = list(deps) + ([] if previous is None else [previous])
     aliases = {} if previous is None else {4 + len(blocks) + len(deps): 0}
     return pl.pallas_call(
         body,
-        out_shape=jax.ShapeDtypeStruct((micro_count, tokens, dim), jnp.bfloat16),
+        out_shape=jax.ShapeDtypeStruct((micro_count, each, dim), jnp.bfloat16),
         grid=(core_steps + dim // cols,),
         in_specs=[core_spec, core_spec, core_spec, pl.BlockSpec((width, cols), lambda s: (0, tail(s)))]
         + [pl.BlockSpec((size, cols), lambda s: (0, tail(s))) for size in sizes] + [ANY] * len(extra),
-        out_specs=pl.BlockSpec((1, tokens, cols), lambda s: (micro, 0, tail(s))),
+        out_specs=pl.BlockSpec((micros, each, cols), lambda s: (micro // micros, 0, tail(s))),
         scratch_shapes=[pltpu.VMEM((tokens, width), jnp.bfloat16)],
         input_output_aliases=aliases,
         compiler_params=pltpu.CompilerParams(vmem_limit_bytes=VMEM_LIMIT),
@@ -391,8 +392,9 @@
             normed = normalize([piece for m in micros for piece in pieces[m]], norm_attn, deps)
             return [jnp.dot(normed, flat(weight), preferred_element_type=jnp.float32).astype(jnp.bfloat16) for weight in (w_query, w_key, w_value)]
 
-        def mix(m, row_block, projected, previous, deps):
-            return attend(*projected, row_block, pieces[m], w_out[0].reshape(heads_width, dim), m, micro_count, seq_len, w_query.shape[3], previous, deps)
+        def mix(micros, projected, previous, deps):
+            blocks = [piece for m in micros for piece in pieces[m]]
+            return attend(*projected, blocks, w_out[0].reshape(heads_width, dim), micros[0], tokens, micro_count, seq_len, w_query.shape[3], previous, deps)
 
         here[0] = own(0, (shared[0],))
         last = finish(0, 0, (here[0][0],))
@@ -406,15 +408,14 @@
         both = project((0, 1), (here[3][0],))
         last = finish(2, 0, (both[2],))
         last = finish(2, 1, (*both, *last))
-        out = mix(0, 0, both, None, last)
-        out = mix(1, 1, both, out, ())
+        out = mix((0, 1), both, None, last)
         last = finish(3, 0, (out,))
         third = project((2,), last)
         last = finish(3, 1, (third[2],))
         last = finish(3, 2, (third[1], *last))
-        out = mix(2, 0, third, out, last)
+        out = mix((2,), third, out, last)
         fourth = project((3,), (out,))
-        out = mix(3, 0, fourth, out, ())
+        out = mix((3,), fourth, out, ())
         return out.reshape(residual.shape)
 
     in_specs = (tok_spec,) * 5 + (vec_spec, mat_spec, mat_spec, mat_spec, vec_spec, head_spec, head_spec, head_spec, head_spec)

time: 809 us -> 803 us (level)
    pallas_call x4 -> x3, Pallas kernels: 101 us -> 94.6 us  [attend(): pl.pallas_call(body, out_shape=jax.ShapeDtypeStruct((micro_count, each, d...]
  transfers between devices with their start and end apart: 27 -> 27, of which waited for: 8 -> 8; matrix products, arithmetic and copies ran while one was open for 23% -> 23% of each run, Pallas kernels for 51% -> 50%
where the time goes in v3:
time: 803 us; the launch traced here: 795 us
  Pallas kernels  436 us (54%)
  matrix products  228 us (28%)
  waiting for transfers between devices  85.9 us (11%)
  starting transfers between devices  25.8 us (3%)
  local copies, waits for them, and re-layouts  16.1 us (2%)
    dot_general x9, matrix products, project(): jnp.dot(normed, flat(weight), preferred_element_type=jnp.float32)  228 us
    pallas_call x8, Pallas kernels, chip_partial(): pl.pallas_call(body, out_shape=[jax.ShapeDtypeStruct((parts * count * til...  103 us
    pallas_call x3, Pallas kernels, attend(): pl.pallas_call(body, out_shape=jax.ShapeDtypeStruct((micro_count, each, d...  94.6 us
    pallas_call x2, Pallas kernels, gated_hidden(): pl.pallas_call(gated, out_shape=jax.ShapeDtypeStruct((rows, width), jnp.b...  92.5 us
    ppermute x9, waiting for transfers between devices, finish(): pieces[m].append(lax.ppermute(combined, 'pp', shift_pairs))  49.2 us
    pallas_call x2, Pallas kernels, down_product(): pl.pallas_call(down, out_shape=jax.ShapeDtypeStruct((rows, dim), jnp.bflo...  46.7 us
    pallas_call x9, Pallas kernels, combine_chunk(): pl.pallas_call(body, out_shape=jax.ShapeDtypeStruct((chunk, dim), jnp.bfl...  42 us
    pallas_call x5, Pallas kernels, pick_rows(): pl.pallas_call(body, out_shape=[jax.ShapeDtypeStruct((experts, cap, dim),...  37.9 us
  transfers between devices with their start and end apart: 27, of which 8 were waited for; matrix products, arithmetic and copies ran while one was open for 23% of the time, Pallas kernels for 50%

profile of v3, /device:TPU:0, one launch (start us, length us, event | category | flops | bytes accessed | tf_op | source)
XLA Modules:
  0.0 794.9 jit_solution(16121887369461751269)
XLA Ops:
  22.5 12.1 %combine.8.refs_2_ = f32[12288,128]{1,0:T(8,128)} custom-call(s32[1]{0:T(128)} %bitcast.6.owner_ref, s32[2304]{0:T(1024)} %get-tuple-element.55.rows_ref, f32[2304]{0:T(1024)} %get-tuple-element.51.gates_ref, bf16[1,4,32,96,4096]{4,3,2,1,0:T(8,128)(2,1)} %rest_1_.15, bf16[1,4,32,96,4096]{4,3,2,1,0:T(8,128)(2,1)} %rest_1_.15, ...), custom_call_target="tpu_custom_call" | custom-call | flops 8000000000 | bytes 18874368 | tf_op jit(solution)/shard_map/combine/pallas_call | solution.py:261
  34.6 9.3 %pick.7 = (bf16[32,24,4096]{2,1,0:T(8,128)(2,1)}, bf16[32,24,4096]{2,1,0:T(8,128)(2,1)}) custom-call(s32[2]{0:T(128)} %pad_add_fusion.1.owners_ref, bf16[1,4,32,96,4096]{4,3,2,1,0:T(8,128)(2,1)} %rest_1_.15, bf16[1,4,32,96,4096]{4,3,2,1,0:T(8,128)(2,1)} %rest_1_.15, f32[12288,128]{1,0:T(8,128)} %combine.8.refs_2_), custom_call_target="tpu_custom_call" | custom-call | flops 4000000000 | bytes 25165824 | tf_op jit(solution)/shard_map/pick/pallas_call | solution.py:196
  44.0 13.5 %combine.9 = (f32[4096,128]{1,0:T(8,128)}, f32[4096,128]{1,0:T(8,128)}, f32[4096,128]{1,0:T(8,128)}) custom-call(s32[1]{0:T(128)} %bitcast.6.owner_ref, s32[2304]{0:T(1024)} %get-tuple-element.54.rows_ref, f32[2304]{0:T(1024)} %get-tuple-element.50.gates_ref, bf16[1,4,32,96,4096]{4,3,2,1,0:T(8,128)(2,1)} %rest_1_.15, bf16[1,4,32,96,4096]{4,3,2,1,0:T(8,128)(2,1)} %rest_1_.15, ...), custom_call_target="tpu_custom_call" | custom-call | flops 8000000000 | bytes 18874368 | tf_op jit(solution)/shard_map/combine/pallas_call | solution.py:261
  57.5 9.5 %pick.8 = (bf16[32,24,4096]{2,1,0:T(8,128)(2,1)}, bf16[32,24,4096]{2,1,0:T(8,128)(2,1)}) custom-call(s32[2]{0:T(128)} %pad_add_fusion.1.owners_ref, bf16[1,4,32,96,4096]{4,3,2,1,0:T(8,128)(2,1)} %rest_1_.15, bf16[1,4,32,96,4096]{4,3,2,1,0:T(8,128)(2,1)} %rest_1_.15, f32[4096,128]{1,0:T(8,128)} %get-tuple-element.29.refs_2_), custom_call_target="tpu_custom_call" | custom-call | flops 4000000000 | bytes 25165824 | tf_op jit(solution)/shard_map/pick/pallas_call | solution.py:196
  77.2 12.6 %combine.10 = (f32[6144,128]{1,0:T(8,128)}, f32[6144,128]{1,0:T(8,128)}) custom-call(s32[1]{0:T(128)} %bitcast.6.owner_ref, s32[2304]{0:T(1024)} %get-tuple-element.56.rows_ref, f32[2304]{0:T(1024)} %get-tuple-element.52.gates_ref, bf16[1,4,32,96,4096]{4,3,2,1,0:T(8,128)(2,1)} %rest_1_.15, bf16[1,4,32,96,4096]{4,3,2,1,0:T(8,128)(2,1)} %rest_1_.15, ...), custom_call_target="tpu_custom_call" | custom-call | flops 8000000000 | bytes 18874368 | tf_op jit(solution)/shard_map/combine/pallas_call | solution.py:261
  89.8 9.4 %pick.9 = (bf16[32,24,4096]{2,1,0:T(8,128)(2,1)}, bf16[32,24,4096]{2,1,0:T(8,128)(2,1)}) custom-call(s32[2]{0:T(128)} %pad_add_fusion.owners_ref, bf16[1,4,32,96,4096]{4,3,2,1,0:T(8,128)(2,1)} %rest_1_.15, bf16[1,4,32,96,4096]{4,3,2,1,0:T(8,128)(2,1)} %rest_1_.15, f32[6144,128]{1,0:T(8,128)} %get-tuple-element.31.refs_2_), custom_call_target="tpu_custom_call" | custom-call | flops 4000000000 | bytes 25165824 | tf_op jit(solution)/shard_map/pick/pallas_call | solution.py:196
  101.1 13.5 %combine.11 = (f32[4096,128]{1,0:T(8,128)}, f32[4096,128]{1,0:T(8,128)}, f32[4096,128]{1,0:T(8,128)}) custom-call(s32[1]{0:T(128)} %bitcast.6.owner_ref, s32[2304]{0:T(1024)} %get-tuple-element.53.rows_ref, f32[2304]{0:T(1024)} %get-tuple-element.49.gates_ref, bf16[1,4,32,96,4096]{4,3,2,1,0:T(8,128)(2,1)} %rest_1_.15, ...), custom_call_target="tpu_custom_call" | custom-call | flops 8000000000 | bytes 18874368 | tf_op jit(solution)/shard_map/combine/pallas_call | solution.py:261
  114.6 46.5 %gated.2.hidden_ref = bf16[768,2816]{1,0:T(8,128)(2,1)} custom-call(bf16[1536,4096]{1,0:T(8,128)(2,1)} %bitcast.122, f32[1,4096]{1,0:T(1,128)} %gain_ref.3, bf16[4096,2816]{1,0:T(8,128)(2,1)} %bitcast.147, bf16[4096,2816]{1,0:T(8,128)(2,1)} %bitcast.149, f32[4096,128]{1,0:T(8,128)} %get-tuple-element.34.rest_0_), custom_call_target="tpu_custom_call" | custom-call | flops 35433480192 | bytes 46137344 | tf_op jit(solution)/shard_map/gated/pallas_call | solution.py:77
  161.1 23.3 %down.2.rest_4_.sh_ref = bf16[768,4096]{1,0:T(8,128)(2,1)} custom-call(bf16[768,2816]{1,0:T(8,128)(2,1)} %gated.2.hidden_ref, bf16[2816,4096]{1,0:T(8,128)(2,1)} %bitcast.151), custom_call_target="tpu_custom_call" | custom-call | flops 17716740096 | bytes 23068672 | tf_op jit(solution)/shard_map/down/pallas_call | solution.py:111
  184.4 12.2 %combine.12.own_ref.rest_0_ = f32[12288,128]{1,0:T(8,128)} custom-call(s32[1]{0:T(128)} %bitcast.owner_ref, s32[2304]{0:T(1024)} %squeeze.91.rows_ref, f32[2304]{0:T(1024)} %squeeze.92.gates_ref, bf16[1,4,32,96,4096]{4,3,2,1,0:T(8,128)(2,1)} %rest_1_.15, bf16[1,4,32,96,4096]{4,3,2,1,0:T(8,128)(2,1)} %rest_1_.15, ...), custom_call_target="tpu_custom_call" | custom-call | flops 8000000000 | bytes 18874368 | tf_op jit(solution)/shard_map/combine/pallas_call | solution.py:261
  196.6 16.8 %collective-permute-done.8.far_ref = f32[12288,128]{1,0:T(8,128)} collective-permute-done((f32[12288,128]{1,0:T(8,128)}, f32[12288,128]{1,0:T(8,128)}, u32[]{:S(2)}, u32[]{:S(2)}) %collective-permute-start.8) | collective-permute-done | bytes 6291488 | tf_op jit(solution)/shard_map/ppermute | solution.py:365
  213.4 8.5 %finish.9.rest_0_ = bf16[384,4096]{1,0:T(8,128)(2,1)} custom-call(f32[12288,128]{1,0:T(8,128)} %combine.12.own_ref.rest_0_, f32[12288,128]{1,0:T(8,128)} %collective-permute-done.8.far_ref, bf16[1536,4096]{1,0:T(8,128)(2,1)} %bitcast.123, bf16[768,4096]{1,0:T(8,128)(2,1)} %down.2.rest_4_.sh_ref, f32[12288,128]{1,0:T(8,128)} %combine.12.own_ref.rest_0_), custom_call_target="tpu_custom_call" | custom-call | flops 1000000000 | bytes 22020096 | tf_op jit(solution)/shard_map/finish/pallas_call | solution.py:300
  221.9 46.0 %gated.3.rest_4_.hidden_ref = bf16[768,2816]{1,0:T(8,128)(2,1)} custom-call(bf16[1536,4096]{1,0:T(8,128)(2,1)} %bitcast.124, f32[1,4096]{1,0:T(1,128)} %gain_ref.3, bf16[4096,2816]{1,0:T(8,128)(2,1)} %bitcast.148, bf16[4096,2816]{1,0:T(8,128)(2,1)} %bitcast.150, bf16[384,4096]{1,0:T(8,128)(2,1)} %finish.9.rest_0_), custom_call_target="tpu_custom_call" | custom-call | flops 35433480192 | bytes 46137344 | tf_op jit(solution)/shard_map/gated/pallas_call | solution.py:77
  269.8 13.5 %combine.13 = (f32[4096,128]{1,0:T(8,128)}, f32[4096,128]{1,0:T(8,128)}, f32[4096,128]{1,0:T(8,128)}) custom-call(s32[1]{0:T(128)} %bitcast.owner_ref, s32[2304]{0:T(1024)} %squeeze.87.rows_ref, f32[2304]{0:T(1024)} %squeeze.88.gates_ref, bf16[1,4,32,96,4096]{4,3,2,1,0:T(8,128)(2,1)} %rest_1_.15, bf16[1,4,32,96,4096]{4,3,2,1,0:T(8,128)(2,1)} %rest_1_.15, ...), custom_call_target="tpu_custom_call" | custom-call | flops 8000000000 | bytes 18874368 | tf_op jit(solution)/shard_map/combine/pallas_call | solution.py:261
  288.7 14.6 %collective-permute-done.11.far_ref = f32[4096,128]{1,0:T(8,128)} collective-permute-done((f32[4096,128]{1,0:T(8,128)}, f32[4096,128]{1,0:T(8,128)}, u32[]{:S(2)}, u32[]{:S(2)}) %collective-permute-start.11) | collective-permute-done | bytes 2097184 | tf_op jit(solution)/shard_map/ppermute | solution.py:365
  309.0 23.4 %down.3.rest_4_.sh_ref = bf16[768,4096]{1,0:T(8,128)(2,1)} custom-call(bf16[768,2816]{1,0:T(8,128)(2,1)} %gated.3.rest_4_.hidden_ref, bf16[2816,4096]{1,0:T(8,128)(2,1)} %bitcast.152, bf16[128,4096]{1,0:T(8,128)(2,1)} %finish.11.rest_0_), custom_call_target="tpu_custom_call" | custom-call | flops 17716740096 | bytes 23068672 | tf_op jit(solution)/shard_map/down/pallas_call | solution.py:111
  332.6 12.6 %combine.14 = (f32[6144,128]{1,0:T(8,128)}, f32[6144,128]{1,0:T(8,128)}) custom-call(s32[1]{0:T(128)} %bitcast.owner_ref, s32[2304]{0:T(1024)} %squeeze.96.rows_ref, f32[2304]{0:T(1024)} %squeeze.97.gates_ref, bf16[1,4,32,96,4096]{4,3,2,1,0:T(8,128)(2,1)} %rest_1_.15, bf16[1,4,32,96,4096]{4,3,2,1,0:T(8,128)(2,1)} %rest_1_.15, ...), custom_call_target="tpu_custom_call" | custom-call | flops 8000000000 | bytes 18874368 | tf_op jit(solution)/shard_map/combine/pallas_call | solution.py:261
  356.3 13.6 %combine.15 = (f32[4096,128]{1,0:T(8,128)}, f32[4096,128]{1,0:T(8,128)}, f32[4096,128]{1,0:T(8,128)}) custom-call(s32[1]{0:T(128)} %bitcast.owner_ref, s32[2304]{0:T(1024)} %squeeze.76.rows_ref, f32[2304]{0:T(1024)} %squeeze.78.gates_ref, bf16[1,4,32,96,4096]{4,3,2,1,0:T(8,128)(2,1)} %rest_1_.15, bf16[1,4,32,96,4096]{4,3,2,1,0:T(8,128)(2,1)} %rest_1_.15, ...), custom_call_target="tpu_custom_call" | custom-call | flops 8000000000 | bytes 18874368 | tf_op jit(solution)/shard_map/combine/pallas_call | solution.py:261
  377.1 22.3 %collective-permute-done.15.refs_1_.rest_1_ = bf16[128,4096]{1,0:T(8,128)(2,1)S(1)} collective-permute-done((bf16[128,4096]{1,0:T(8,128)(2,1)S(1)}, bf16[128,4096]{1,0:T(8,128)(2,1)S(1)}, u32[]{:S(2)}, u32[]{:S(2)}) %collective-permute-start.15) | collective-permute-done | bytes 1048608 | tf_op jit(solution)/shard_map/ppermute | solution.py:388
  401.4 19.8 %collective-permute-done.17.refs_3_.rest_3_ = bf16[128,4096]{1,0:T(8,128)(2,1)} collective-permute-done((bf16[128,4096]{1,0:T(8,128)(2,1)}, bf16[128,4096]{1,0:T(8,128)(2,1)}, u32[]{:S(2)}, u32[]{:S(2)}) %collective-permute-start.17) | collective-permute-done | bytes 1048608 | tf_op jit(solution)/shard_map/ppermute | solution.py:388
  430.0 33.2 %fusion.33.rest_0_.rest_2_.v_ref = bf16[768,4096]{1,0:T(8,128)(2,1)} fusion(bf16[768,4096]{1,0:T(8,128)(2,1)} %normalize.3, bf16[512,8,32,128]{3,2,1,0:T(8,128)(2,1)} %bitcast.138), kind=kOutput, calls=%fused_computation.29 | convolution fusion | flops 25772949504 | bytes 46137344 | tf_op jit(solution)/shard_map/dot_general | solution.py:393
  470.1 35.7 %fusion.30.rest_1_.k_ref = bf16[768,4096]{1,0:T(8,128)(2,1)} fusion(bf16[768,4096]{1,0:T(8,128)(2,1)} %normalize.3, bf16[512,8,32,128]{3,2,1,0:T(8,128)(2,1)} %bitcast.141), kind=kOutput, calls=%fused_computation.28 | convolution fusion | flops 25772949504 | bytes 46137344 | tf_op jit(solution)/shard_map/dot_general | solution.py:393
  505.8 31.4 %fusion.27.rest_0_.q_ref = bf16[768,4096]{1,0:T(8,128)(2,1)} fusion(bf16[768,4096]{1,0:T(8,128)(2,1)S(1)} %bitcast.137, bf16[512,8,32,128]{3,2,1,0:T(8,128)(2,1)} %bitcast.144), kind=kOutput, calls=%fused_computation.27 | convolution fusion | flops 25772949504 | bytes 46137344 | tf_op jit(solution)/shard_map/dot_general | solution.py:393
  543.8 44.4 %attend.3.rest_0_.rest_3_ = bf16[4,384,4096]{2,1,0:T(8,128)(2,1)} custom-call(bf16[768,4096]{1,0:T(8,128)(2,1)} %fusion.27.rest_0_.q_ref, bf16[768,4096]{1,0:T(8,128)(2,1)} %fusion.30.rest_1_.k_ref, bf16[768,4096]{1,0:T(8,128)(2,1)} %fusion.33.rest_0_.rest_2_.v_ref, bf16[4096,4096]{1,0:T(8,128)(2,1)} %bitcast.133, ...), custom_call_target="tpu_custom_call" | custom-call | flops 25769803776 | bytes 33554432 | tf_op jit(solution)/shard_map/attend/pallas_call | solution.py:169
  599.9 21.8 %fusion.42.rest_0_.k_ref = bf16[384,4096]{1,0:T(8,128)(2,1)} fusion(bf16[384,4096]{1,0:T(8,128)(2,1)} %normalize.4, bf16[512,8,32,128]{3,2,1,0:T(8,128)(2,1)} %bitcast.142), kind=kOutput, calls=%fused_computation.32 | convolution fusion | flops 12886474752 | bytes 39845888 | tf_op jit(solution)/shard_map/dot_general | solution.py:393
  621.7 21.5 %fusion.48.rest_0_.v_ref = bf16[384,4096]{1,0:T(8,128)(2,1)} fusion(bf16[384,4096]{1,0:T(8,128)(2,1)} %normalize.4, bf16[512,8,32,128]{3,2,1,0:T(8,128)(2,1)} %bitcast.139), kind=kOutput, calls=%fused_computation.34 | convolution fusion | flops 12886474752 | bytes 39845888 | tf_op jit(solution)/shard_map/dot_general | solution.py:393
  647.3 21.5 %fusion.36.q_ref = bf16[384,4096]{1,0:T(8,128)(2,1)} fusion(bf16[384,4096]{1,0:T(8,128)(2,1)} %normalize.4, bf16[512,8,32,128]{3,2,1,0:T(8,128)(2,1)} %bitcast.145), kind=kOutput, calls=%fused_computation.30 | convolution fusion | flops 12886474752 | bytes 39845888 | tf_op jit(solution)/shard_map/dot_general | solution.py:393
  674.4 25.1 %attend.4.refs_4_.rest_3_ = bf16[4,384,4096]{2,1,0:T(8,128)(2,1)} custom-call(bf16[384,4096]{1,0:T(8,128)(2,1)} %fusion.36.q_ref, bf16[384,4096]{1,0:T(8,128)(2,1)} %fusion.42.rest_0_.k_ref, bf16[384,4096]{1,0:T(8,128)(2,1)} %fusion.48.rest_0_.v_ref, bf16[4096,4096]{1,0:T(8,128)(2,1)} %bitcast.134, ...), custom_call_target="tpu_custom_call", output_to_operand_aliasing={{}: (7, {})} | custom-call | flops 12884901888 | bytes 33554432 | tf_op jit(solution)/shard_map/attend/pallas_call | solution.py:169
  706.8 21.5 %fusion.51.v_ref = bf16[384,4096]{1,0:T(8,128)(2,1)} fusion(bf16[384,4096]{1,0:T(8,128)(2,1)} %normalize.5, bf16[512,8,32,128]{3,2,1,0:T(8,128)(2,1)} %bitcast.140), kind=kOutput, calls=%fused_computation.35 | convolution fusion | flops 12886474752 | bytes 39845888 | tf_op jit(solution)/shard_map/dot_general | solution.py:393
  728.3 20.8 %fusion.45.k_ref = bf16[384,4096]{1,0:T(8,128)(2,1)} fusion(bf16[384,4096]{1,0:T(8,128)(2,1)S(1)} %copy-done.4, bf16[512,8,32,128]{3,2,1,0:T(8,128)(2,1)} %bitcast.143), kind=kOutput, calls=%fused_computation.33 | convolution fusion | flops 12886474752 | bytes 39845888 | tf_op jit(solution)/shard_map/dot_general | solution.py:393
  749.1 20.6 %fusion.39.q_ref = bf16[384,4096]{1,0:T(8,128)(2,1)} fusion(bf16[384,4096]{1,0:T(8,128)(2,1)S(1)} %copy-done.4, bf16[512,8,32,128]{3,2,1,0:T(8,128)(2,1)} %bitcast.146), kind=kOutput, calls=%fused_computation.31 | convolution fusion | flops 12886474752 | bytes 39845888 | tf_op jit(solution)/shard_map/dot_general | solution.py:393
  769.6 25.1 %attend.5 = bf16[4,384,4096]{2,1,0:T(8,128)(2,1)} custom-call(bf16[384,4096]{1,0:T(8,128)(2,1)} %fusion.39.q_ref, bf16[384,4096]{1,0:T(8,128)(2,1)} %fusion.45.k_ref, bf16[384,4096]{1,0:T(8,128)(2,1)} %fusion.51.v_ref, bf16[4096,4096]{1,0:T(8,128)(2,1)} %bitcast.135, bf16[128,4096]{1,0:T(8,128)(2,1)} %copy-done.1, ...), custom_call_target="tpu_custom_call", output_to_operand_aliasing={{}: (7, {})} | custom-call | flops 12884901888 | bytes 33554432 | tf_op jit(solution)/shard_map/attend/pallas_call | solution.py:169
  (132 shorter events, 119.1 us)
Async XLA Ops:
  4.8 17.7 %collective-permute-start.1 = (bf16[32,24,4096]{2,1,0:T(8,128)(2,1)}, bf16[32,24,4096]{2,1,0:T(8,128)(2,1)}, u32[]{:S(2)}, u32[]{:S(2)}) collective-permute-start(bf16[32,24,4096]{2,1,0:T(8,128)(2,1)} %pick.5.refs_1_), channel_id=1, source_target_pairs={{0,1},{1,0},{2,3},{3,2},{4,5},{5,4},{6,7},{7,6}} | collective-permute-start | bytes 18874376 | tf_op jit(solution)/shard_map/ppermute | solution.py:355
  10.4 33.6 %collective-permute-start.3 = (bf16[32,24,4096]{2,1,0:T(8,128)(2,1)}, bf16[32,24,4096]{2,1,0:T(8,128)(2,1)}, u32[]{:S(2)}, u32[]{:S(2)}) collective-permute-start(bf16[32,24,4096]{2,1,0:T(8,128)(2,1)} %pick.6.rest_4_), channel_id=1, source_target_pairs={{0,1},{1,0},{2,3},{3,2},{4,5},{5,4},{6,7},{7,6}} | collective-permute-start | bytes 18874376 | tf_op jit(solution)/shard_map/ppermute | solution.py:355
  15.7 5.4 collective-permute-start
  44.0 32.7 %collective-permute-start.2 = (bf16[32,24,4096]{2,1,0:T(8,128)(2,1)}, bf16[32,24,4096]{2,1,0:T(8,128)(2,1)}, u32[]{:S(2)}, u32[]{:S(2)}) collective-permute-start(bf16[32,24,4096]{2,1,0:T(8,128)(2,1)} %get-tuple-element.27), channel_id=1, source_target_pairs={{0,1},{1,0},{2,3},{3,2},{4,5},{5,4},{6,7},{7,6}} | collective-permute-start | bytes 18874376 | tf_op jit(solution)/shard_map/ppermute | solution.py:355
  67.0 32.2 %collective-permute-start.7 = (bf16[32,24,4096]{2,1,0:T(8,128)(2,1)}, bf16[32,24,4096]{2,1,0:T(8,128)(2,1)}, u32[]{:S(2)}, u32[]{:S(2)}) collective-permute-start(bf16[32,24,4096]{2,1,0:T(8,128)(2,1)} %get-tuple-element.33), channel_id=1, source_target_pairs={{0,1},{1,0},{2,3},{3,2},{4,5},{5,4},{6,7},{7,6}} | collective-permute-start | bytes 18874376 | tf_op jit(solution)/shard_map/ppermute | solution.py:355
  74.7 138.7 %collective-permute-start.8 = (f32[12288,128]{1,0:T(8,128)}, f32[12288,128]{1,0:T(8,128)}, u32[]{:S(2)}, u32[]{:S(2)}) collective-permute-start(f32[12288,128]{1,0:T(8,128)} %combine.8.refs_2_), channel_id=1, source_target_pairs={{0,2},{1,3},{2,0},{3,1},{4,6},{5,7},{6,4},{7,5}} | collective-permute-start | bytes 18874376 | tf_op jit(solution)/shard_map/ppermute | solution.py:365
  76.6 206.7 %collective-permute-start.12 = (f32[4096,128]{1,0:T(8,128)}, f32[4096,128]{1,0:T(8,128)}, u32[]{:S(2)}, u32[]{:S(2)}) collective-permute-start(f32[4096,128]{1,0:T(8,128)} %get-tuple-element.29.refs_2_), channel_id=1, source_target_pairs={{0,2},{1,3},{2,0},{3,1},{4,6},{5,7},{6,4},{7,5}} | collective-permute-start | bytes 6291464 | tf_op jit(solution)/shard_map/ppermute | solution.py:365
  76.7 107.7 %collective-permute-start.6 = (bf16[32,24,4096]{2,1,0:T(8,128)(2,1)}, bf16[32,24,4096]{2,1,0:T(8,128)(2,1)}, u32[]{:S(2)}, u32[]{:S(2)}) collective-permute-start(bf16[32,24,4096]{2,1,0:T(8,128)(2,1)} %get-tuple-element.28.rest_4_), channel_id=1, source_target_pairs={{0,1},{1,0},{2,3},{3,2},{4,5},{5,4},{6,7},{7,6}} | collective-permute-start | bytes 18874376 | tf_op jit(solution)/shard_map/ppermute | solution.py:355
  76.7 191.2 %collective-permute-start.5 = (bf16[32,24,4096]{2,1,0:T(8,128)(2,1)}, bf16[32,24,4096]{2,1,0:T(8,128)(2,1)}, u32[]{:S(2)}, u32[]{:S(2)}) collective-permute-start(bf16[32,24,4096]{2,1,0:T(8,128)(2,1)} %get-tuple-element.30.rest_4_), channel_id=1, source_target_pairs={{0,1},{1,0},{2,3},{3,2},{4,5},{5,4},{6,7},{7,6}} | collective-permute-start | bytes 18874376 | tf_op jit(solution)/shard_map/ppermute | solution.py:355
  99.2 204.0 %collective-permute-start.11 = (f32[4096,128]{1,0:T(8,128)}, f32[4096,128]{1,0:T(8,128)}, u32[]{:S(2)}, u32[]{:S(2)}) collective-permute-start(f32[4096,128]{1,0:T(8,128)} %get-tuple-element.39), channel_id=1, source_target_pairs={{0,2},{1,3},{2,0},{3,1},{4,6},{5,7},{6,4},{7,5}} | collective-permute-start | bytes 6291464 | tf_op jit(solution)/shard_map/ppermute | solution.py:365
  184.4 148.0 %collective-permute-start.10 = (bf16[32,24,4096]{2,1,0:T(8,128)(2,1)}, bf16[32,24,4096]{2,1,0:T(8,128)(2,1)}, u32[]{:S(2)}, u32[]{:S(2)}) collective-permute-start(bf16[32,24,4096]{2,1,0:T(8,128)(2,1)} %get-tuple-element.37), channel_id=1, source_target_pairs={{0,1},{1,0},{2,3},{3,2},{4,5},{5,4},{6,7},{7,6}} | collective-permute-start | bytes 18874376 | tf_op jit(solution)/shard_map/ppermute | solution.py:355
  213.4 141.5 %collective-permute-start.4 = (bf16[32,24,4096]{2,1,0:T(8,128)(2,1)}, bf16[32,24,4096]{2,1,0:T(8,128)(2,1)}, u32[]{:S(2)}, u32[]{:S(2)}) collective-permute-start(bf16[32,24,4096]{2,1,0:T(8,128)(2,1)} %get-tuple-element.32.rest_4_), channel_id=1, source_target_pairs={{0,1},{1,0},{2,3},{3,2},{4,5},{5,4},{6,7},{7,6}} | collective-permute-start | bytes 18874376 | tf_op jit(solution)/shard_map/ppermute | solution.py:355
  267.9 79.5 %collective-permute-start.9 = (f32[4096,128]{1,0:T(8,128)}, f32[4096,128]{1,0:T(8,128)}, u32[]{:S(2)}, u32[]{:S(2)}) collective-permute-start(f32[4096,128]{1,0:T(8,128)} %get-tuple-element.36), channel_id=1, source_target_pairs={{0,2},{1,3},{2,0},{3,1},{4,6},{5,7},{6,4},{7,5}} | collective-permute-start | bytes 6291464 | tf_op jit(solution)/shard_map/ppermute | solution.py:365
  283.2 116.3 %collective-permute-start.14 = (bf16[384,4096]{1,0:T(8,128)(2,1)}, bf16[384,4096]{1,0:T(8,128)(2,1)}, u32[]{:S(2)}, u32[]{:S(2)}) collective-permute-start(bf16[384,4096]{1,0:T(8,128)(2,1)} %finish.9.rest_0_), channel_id=1, source_target_pairs={{0,4},{4,0},{1,5},{5,1},{2,6},{6,2},{3,7},{7,3}} | collective-permute-start | bytes 9437192 | tf_op jit(solution)/shard_map/ppermute | solution.py:388
  307.1 25.3 %copy-start.3 = (bf16[128,4096]{1,0:T(8,128)(2,1)S(1)}, bf16[128,4096]{1,0:T(8,128)(2,1)}, u32[]{:S(2)}) copy-start(bf16[128,4096]{1,0:T(8,128)(2,1)} %finish.10.rest_0_) | copy-start | bytes 3145732
  307.1 69.8 %collective-permute-start.16 = (bf16[128,4096]{1,0:T(8,128)(2,1)}, bf16[128,4096]{1,0:T(8,128)(2,1)S(1)}, u32[]{:S(2)}, u32[]{:S(2)}) collective-permute-start(bf16[128,4096]{1,0:T(8,128)(2,1)} %finish.11.rest_0_), channel_id=1, source_target_pairs={{0,4},{4,0},{1,5},{5,1},{2,6},{6,2},{3,7},{7,3}} | collective-permute-start | bytes 3145736 | tf_op jit(solution)/shard_map/ppermute | solution.py:388
  332.4 67.0 %collective-permute-start.15 = (bf16[128,4096]{1,0:T(8,128)(2,1)S(1)}, bf16[128,4096]{1,0:T(8,128)(2,1)S(1)}, u32[]{:S(2)}, u32[]{:S(2)}) collective-permute-start(bf16[128,4096]{1,0:T(8,128)(2,1)S(1)} %copy-done.3), channel_id=1, source_target_pairs={{0,4},{4,0},{1,5},{5,1},{2,6},{6,2},{3,7},{7,3}} | collective-permute-start | bytes 3145736 | tf_op jit(solution)/shard_map/ppermute | solution.py:388
  351.3 69.9 %collective-permute-start.17 = (bf16[128,4096]{1,0:T(8,128)(2,1)}, bf16[128,4096]{1,0:T(8,128)(2,1)}, u32[]{:S(2)}, u32[]{:S(2)}) collective-permute-start(bf16[128,4096]{1,0:T(8,128)(2,1)} %finish.12.rest_4_), channel_id=1, source_target_pairs={{0,4},{4,0},{1,5},{5,1},{2,6},{6,2},{3,7},{7,3}} | collective-permute-start | bytes 3145736 | tf_op jit(solution)/shard_map/ppermute | solution.py:388
  354.8 108.4 %collective-permute-start.19 = (f32[6144,128]{1,0:T(8,128)}, f32[6144,128]{1,0:T(8,128)}, u32[]{:S(2)}, u32[]{:S(2)}) collective-permute-start(f32[6144,128]{1,0:T(8,128)} %get-tuple-element.31.refs_2_), channel_id=1, source_target_pairs={{0,2},{1,3},{2,0},{3,1},{4,6},{5,7},{6,4},{7,5}} | collective-permute-start | bytes 9437192 | tf_op jit(solution)/shard_map/ppermute | solution.py:365
  376.9 44.6 %copy-start.5 = (bf16[128,4096]{1,0:T(8,128)(2,1)}, bf16[128,4096]{1,0:T(8,128)(2,1)S(1)}, u32[]{:S(2)}) copy-start(bf16[128,4096]{1,0:T(8,128)(2,1)S(1)} %collective-permute-done.16.refs_2_.rest_2_) | copy-start | bytes 3145732
  376.9 211.2 %collective-permute-start.13 = (f32[4096,128]{1,0:T(8,128)}, f32[4096,128]{1,0:T(8,128)}, u32[]{:S(2)}, u32[]{:S(2)}) collective-permute-start(f32[4096,128]{1,0:T(8,128)} %get-tuple-element.34.rest_0_), channel_id=1, source_target_pairs={{0,2},{1,3},{2,0},{3,1},{4,6},{5,7},{6,4},{7,5}} | collective-permute-start | bytes 6291464 | tf_op jit(solution)/shard_map/ppermute | solution.py:365
  399.4 22.1 %copy-start.6 = (bf16[128,4096]{1,0:T(8,128)(2,1)}, bf16[128,4096]{1,0:T(8,128)(2,1)S(1)}, u32[]{:S(2)}) copy-start(bf16[128,4096]{1,0:T(8,128)(2,1)S(1)} %collective-permute-done.15.refs_1_.rest_1_) | copy-start | bytes 3145732
  399.4 139.1 %collective-permute-start.18 = (f32[6144,128]{1,0:T(8,128)}, f32[6144,128]{1,0:T(8,128)}, u32[]{:S(2)}, u32[]{:S(2)}) collective-permute-start(f32[6144,128]{1,0:T(8,128)} %get-tuple-element.44), channel_id=1, source_target_pairs={{0,2},{1,3},{2,0},{3,1},{4,6},{5,7},{6,4},{7,5}} | collective-permute-start | bytes 9437192 | tf_op jit(solution)/shard_map/ppermute | solution.py:365
  399.5 243.6 %collective-permute-start.21 = (f32[4096,128]{1,0:T(8,128)}, f32[4096,128]{1,0:T(8,128)}, u32[]{:S(2)}, u32[]{:S(2)}) collective-permute-start(f32[4096,128]{1,0:T(8,128)} %get-tuple-element.46), channel_id=1, source_target_pairs={{0,2},{1,3},{2,0},{3,1},{4,6},{5,7},{6,4},{7,5}} | collective-permute-start | bytes 6291464 | tf_op jit(solution)/shard_map/ppermute | solution.py:365
  421.2 247.5 %collective-permute-start.25 = (f32[4096,128]{1,0:T(8,128)}, f32[4096,128]{1,0:T(8,128)}, u32[]{:S(2)}, u32[]{:S(2)}) collective-permute-start(f32[4096,128]{1,0:T(8,128)} %get-tuple-element.48), channel_id=1, source_target_pairs={{0,2},{1,3},{2,0},{3,1},{4,6},{5,7},{6,4},{7,5}} | collective-permute-start | bytes 6291464 | tf_op jit(solution)/shard_map/ppermute | solution.py:365
  463.2 42.6 %slice-start = ((s8[6291456]{0:T(1024)(128)(4,1)}), s8[2097152]{0:T(1024)(128)(4,1)S(1)}, s32[]{:S(2)}) async-start(s8[6291456]{0:T(1024)(128)(4,1)} %bitcast.136), calls=%async_computation | async-start | bytes 4194304
  468.4 125.4 %collective-permute-start.22 = (bf16[192,4096]{1,0:T(8,128)(2,1)}, bf16[192,4096]{1,0:T(8,128)(2,1)}, u32[]{:S(2)}, u32[]{:S(2)}) collective-permute-start(bf16[192,4096]{1,0:T(8,128)(2,1)} %finish.13.rest_3_), channel_id=1, source_target_pairs={{0,4},{4,0},{1,5},{5,1},{2,6},{6,2},{3,7},{7,3}} | collective-permute-start | bytes 4718600 | tf_op jit(solution)/shard_map/ppermute | solution.py:388
  470.1 35.7 %slice-start.1 = ((s8[6291456]{0:T(1024)(128)(4,1)}), s8[4194304]{0:T(1024)(128)(4,1)S(1)}, s32[]{:S(2)}) async-start(s8[6291456]{0:T(1024)(128)(4,1)} %bitcast.136), calls=%async_computation.1 | async-start | bytes 8388608
  543.5 50.3 %collective-permute-start.23 = (bf16[192,4096]{1,0:T(8,128)(2,1)}, bf16[192,4096]{1,0:T(8,128)(2,1)S(1)}, u32[]{:S(2)}, u32[]{:S(2)}) collective-permute-start(bf16[192,4096]{1,0:T(8,128)(2,1)} %finish.14.rest_4_), channel_id=1, source_target_pairs={{0,4},{4,0},{1,5},{5,1},{2,6},{6,2},{3,7},{7,3}} | collective-permute-start | bytes 4718600 | tf_op jit(solution)/shard_map/ppermute | solution.py:388
  592.1 107.5 %collective-permute-start.20 = (bf16[128,4096]{1,0:T(8,128)(2,1)}, bf16[128,4096]{1,0:T(8,128)(2,1)S(1)}, u32[]{:S(2)}, u32[]{:S(2)}) collective-permute-start(bf16[128,4096]{1,0:T(8,128)(2,1)} %finish.15.refs_3_), channel_id=1, source_target_pairs={{0,4},{4,0},{1,5},{5,1},{2,6},{6,2},{3,7},{7,3}} | collective-permute-start | bytes 3145736 | tf_op jit(solution)/shard_map/ppermute | solution.py:388
  647.0 52.5 %collective-permute-start.24 = (bf16[128,4096]{1,0:T(8,128)(2,1)}, bf16[128,4096]{1,0:T(8,128)(2,1)S(1)}, u32[]{:S(2)}, u32[]{:S(2)}) collective-permute-start(bf16[128,4096]{1,0:T(8,128)(2,1)} %finish.16.rest_1_), channel_id=1, source_target_pairs={{0,4},{4,0},{1,5},{5,1},{2,6},{6,2},{3,7},{7,3}} | collective-permute-start | bytes 3145736 | tf_op jit(solution)/shard_map/ppermute | solution.py:388
  672.6 26.9 %collective-permute-start.26 = (bf16[128,4096]{1,0:T(8,128)(2,1)}, bf16[128,4096]{1,0:T(8,128)(2,1)}, u32[]{:S(2)}, u32[]{:S(2)}) collective-permute-start(bf16[128,4096]{1,0:T(8,128)(2,1)} %finish.17.rest_2_), channel_id=1, source_target_pairs={{0,4},{4,0},{1,5},{5,1},{2,6},{6,2},{3,7},{7,3}} | collective-permute-start | bytes 3145736 | tf_op jit(solution)/shard_map/ppermute | solution.py:388
  (11 other events, 76.5 us)
